TPU v7x, 32 devices: a whole 2x2x4 slice. The times are simulated.
32 devices in a mesh: ctx: 16 (over z, y, core), wsh: 2 (over x).
Axes of the slice: x: 2, y: 2, z: 4, core: 2. Of those that a mesh axis runs over, the one named last changes fastest.
Arguments:
- tokens: bfloat16 [4, 2048, 1152], P('wsh', 'ctx'), may hold values from -6 to 6
- block_order: int32 [16], replicated, may hold values from 0 to 15, each once
- gain_attn_pre: bfloat16 [1152], P('wsh'), may hold values from 0.25 to 1.75
- gain_query: bfloat16 [256], P('wsh'), may hold values from 0.25 to 1.75
- gain_key: bfloat16 [256], P('wsh'), may hold values from 0.25 to 1.75
- gain_attn_post: bfloat16 [1152], P('wsh'), may hold values from 0.25 to 1.75
- gain_ff_pre: bfloat16 [1152], P('wsh'), may hold values from 0.25 to 1.75
- gain_ff_post: bfloat16 [1152], P('wsh'), may hold values from 0.25 to 1.75
- weight_query: bfloat16 [1152, 1024], P(None, 'wsh'), may hold values from -0.1875 to 0.1875
- weight_key: bfloat16 [1152, 256], P(None, 'wsh'), may hold values from -0.1875 to 0.1875
- weight_value: bfloat16 [1152, 256], P(None, 'wsh'), may hold values from -0.1875 to 0.1875
- weight_out: bfloat16 [1024, 1152], P(None, 'wsh'), may hold values from -0.1875 to 0.1875
- weight_gate: bfloat16 [1152, 6912], P(None, 'wsh'), may hold values from -0.1875 to 0.1875
- weight_up: bfloat16 [1152, 6912], P(None, 'wsh'), may hold values from -0.1875 to 0.1875
- weight_down: bfloat16 [1152, 6912], P(None, 'wsh'), may hold values from -0.078125 to 0.078125
- cotangent: bfloat16 [4, 2048, 1152], P('wsh', 'ctx'), may hold values from -6 to 6
Outputs:
- output: bfloat16 [4, 2048, 1152], P('wsh', 'ctx')
- grad_tokens: float32 [4, 2048, 1152], P('wsh', 'ctx')
- grad_gain_attn_pre: float32 [1152], P(('ctx', 'wsh'))
- grad_gain_query: float32 [256], P(('ctx', 'wsh'))
- grad_gain_key: float32 [256], P(('ctx', 'wsh'))
- grad_gain_attn_post: float32 [1152], P(('ctx', 'wsh'))
- grad_gain_ff_pre: float32 [1152], P(('ctx', 'wsh'))
- grad_gain_ff_post: float32 [1152], P(('ctx', 'wsh'))
- grad_weight_query: float32 [1152, 1024], P('ctx', 'wsh')
- grad_weight_key: float32 [1152, 256], P('ctx', 'wsh')
- grad_weight_value: float32 [1152, 256], P('ctx', 'wsh')
- grad_weight_out: float32 [1024, 1152], P('ctx', 'wsh')
- grad_weight_gate: float32 [1152, 6912], P('ctx', 'wsh')
- grad_weight_up: float32 [1152, 6912], P('ctx', 'wsh')
- grad_weight_down: float32 [1152, 6912], P('ctx', 'wsh')
Inputs may be any that keep to these rules, and one draw needn't show every extreme that they name: block_order is a permutation of 0 to 15.
All inputs are finite; a program needn't handle non-finite values.
Results may differ from a plain program's by a relative error of at most 0.025.
Values may be sent and summed in bfloat16 or wider, within the bound.
A program may use at most 384 MiB of HBM per device.

v0:
```python
import functools
import math

import jax
import jax.numpy as jnp
from jax import lax
from jax.experimental import pallas as pl
from jax.experimental.pallas import tpu as pltpu
from jax.sharding import PartitionSpec as P

EPS = 1e-06
ROPE_BASE = 1000000.0
SCORE_SCALE = 0.0625
F32 = jnp.float32
BF16 = jnp.bfloat16
MESH = pl.DeviceIdType.MESH


def norm_gain(vector, gain):
    return vector * lax.rsqrt(jnp.mean(vector * vector, -1, keepdims=True) + EPS) * gain


def rotate(vector, cosine, sine):
    middle = vector.shape[-1] // 2
    first = vector[..., :middle]
    second = vector[..., middle:]
    return jnp.concatenate([first * cosine - second * sine, second * cosine + first * sine], -1)


def angle_tables(positions, head_size):
    middle = head_size // 2
    inverse = jnp.exp(
        jnp.arange(middle, dtype=F32) * (-2.0 * math.log(ROPE_BASE) / head_size)
    )
    theta = positions.astype(F32)[:, None] * inverse[None, :]
    return (jnp.cos(theta), jnp.sin(theta))


def swap(value):
    return lax.ppermute(value, "wsh", [(0, 1), (1, 0)])


def half_of(value, which):
    middle = value.shape[-1] // 2
    return jnp.where(which == 0, value[..., :middle], value[..., middle:])


def dot(left, right, dims):
    return lax.dot_general(left, right, (dims, ((), ())), preferred_element_type=F32)


def stack_heads(ref, half, block, heads, size):
    rows = slice(half * block, (half + 1) * block)
    return jnp.concatenate([ref[0, rows, h * size : (h + 1) * size] for h in range(heads)], 0)


def attend_backward_kernel(
    heads, chunk, q_ref, kv_ref, g_ref, mix_ref, tot_ref, qpos_ref, kpos_ref, dq_ref, dkv_ref
):
    shards, _, rows, pair = kv_ref.shape
    block, size = rows // 2, pair // 2
    stacked = heads * block
    queries, scaled, correction = [], [], []
    for half in range(2):
        queries.append(stack_heads(q_ref, half, block, heads, size))
        grad = stack_heads(g_ref, half, block, heads, size).astype(F32)
        span = slice(half * stacked, (half + 1) * stacked)
        total = tot_ref[0, span, :1]
        delta = jnp.sum(grad * mix_ref[0, span, :], -1, keepdims=True)
        scaled.append((grad / total).astype(BF16))
        correction.append(delta / total)
    grad_query = [jnp.zeros((stacked, size), F32) for _ in range(2)]
    for first in range(0, shards, chunk):
        span = slice(first * block, (first + chunk) * block)
        for key_half in range(2):
            part = kv_ref[first : first + chunk, 0, key_half * block : (key_half + 1) * block, :]
            part = part.reshape(chunk * block, pair)
            keys, values = part[:, :size], part[:, size:]
            grad_keys = jnp.zeros((chunk * block, size), F32)
            grad_values = jnp.zeros((chunk * block, size), F32)
            for half in range(key_half, 2):
                weights = jnp.exp(dot(queries[half], keys, ((1,), (1,))) * SCORE_SCALE)
                if half == key_half:
                    allowed = (
                        kpos_ref[key_half : key_half + 1, span]
                        <= qpos_ref[half * stacked : (half + 1) * stacked, :]
                    )
                    weights = jnp.where(allowed, weights, 0.0)
                low = weights.astype(BF16)
                grad_weights = dot(scaled[half], values, ((1,), (1,)))
                grad_scores = (weights * (grad_weights - correction[half])).astype(BF16)
                grad_query[half] += dot(grad_scores, keys, ((1,), (0,)))
                grad_keys += dot(grad_scores, queries[half], ((0,), (0,)))
                grad_values += dot(low, scaled[half], ((0,), (0,)))
            both = jnp.concatenate([grad_keys * SCORE_SCALE, grad_values], -1).astype(BF16)
            dkv_ref[first : first + chunk, 0, key_half * block : (key_half + 1) * block, :] = (
                both.reshape(chunk, block, pair)
            )
    for half in range(2):
        for h in range(heads):
            dq_ref[0, half * block : (half + 1) * block, h * size : (h + 1) * size] = (
                grad_query[half][h * block : (h + 1) * block] * SCORE_SCALE
            )


def whole(shape):
    return pl.BlockSpec(shape, lambda s: (0,) * len(shape))


def attend_backward(query_low, pairs, grad_mixed, mixed, totals, query_pos, key_pos, heads):
    sequences, rows, width = query_low.shape
    shards, _, _, pair = pairs.shape
    stacked = query_pos.shape[0]
    row = pl.BlockSpec((1, rows, width), lambda s: (s, 0, 0))
    stack = lambda last: pl.BlockSpec((1, stacked, last), lambda s: (s, 0, 0))
    pairs_spec = pl.BlockSpec((shards, 1, rows, pair), lambda s: (0, s, 0, 0))
    return pl.pallas_call(
        functools.partial(attend_backward_kernel, heads, min(shards, 16)),
        grid=(sequences,),
        in_specs=[
            row,
            pairs_spec,
            row,
            stack(pair // 2),
            stack(128),
            whole(query_pos.shape),
            whole(key_pos.shape),
        ],
        out_specs=[row, pairs_spec],
        out_shape=[
            jax.ShapeDtypeStruct((sequences, rows, width), F32),
            jax.ShapeDtypeStruct(pairs.shape, BF16),
        ],
        name="attend_backward",
    )(query_low, pairs, grad_mixed, mixed, totals, query_pos, key_pos)


class Ring:
    def __init__(self, devices):
        self.chips = devices // 2
        me = lax.axis_index("ctx")
        self.core = me % 2
        chip = me // 2
        across = chip % 2
        deep = chip // 2
        self.place = deep + across * (self.chips - 1 - 2 * deep)
        self.partner = me + 1 - 2 * self.core
        self.right = self.device((self.place + 1) % self.chips, self.core)
        self.left = self.device((self.place + self.chips - 1) % self.chips, self.core)

    def device(self, place, core):
        side = place // (self.chips // 2)
        return 2 * (2 * (place + side * (self.chips - 1 - 2 * place)) + side) + core

    def enter(self, across=False):
        barrier = pltpu.get_barrier_semaphore()
        targets = [{"ctx": other} for other in (self.left, self.right, self.partner)]
        if across:
            targets.append({"wsh": 1 - lax.axis_index("wsh")})
        for target in targets:
            pl.semaphore_signal(barrier, inc=1, device_id=target, device_id_type=MESH)
        pl.semaphore_wait(barrier, len(targets))


def ring_sum_kernel(devices, pieces, arrays, ahead, *refs):
    parts, outs = refs[:arrays], refs[arrays : 2 * arrays]
    own, other, flow = (refs[(2 + i) * arrays : (3 + i) * arrays] for i in range(3))
    own_sem, put_sem, got_sem, send_sem, recv_sem = refs[5 * arrays :]
    ring = Ring(devices)
    chips = ring.chips

    def region(p):
        array, _, first, rows, start, cols = pieces[p]
        return array, pl.ds(first, rows), pl.ds(start, cols)

    def chunk(p, step):
        way = pieces[p][1]
        return (ring.place + 2 * chips + way * (-1 - step)) % chips

    def load(p, step):
        array, rows, cols = region(p)
        source = ring.device(chunk(p, step), ring.core)
        return pltpu.make_async_copy(
            parts[array].at[source, rows, cols],
            own[array].at[step, rows, cols],
            own_sem.at[p, step],
        )

    def give(p, step):
        array, rows, cols = region(p)
        source = ring.device(chunk(p, step), 1 - ring.core)
        return pltpu.make_async_remote_copy(
            src_ref=parts[array].at[source, rows, cols],
            dst_ref=other[array].at[step, rows, cols],
            send_sem=put_sem.at[p, step],
            recv_sem=got_sem.at[p, step],
            device_id={"ctx": ring.partner},
            device_id_type=MESH,
        )

    def pass_on(p, step):
        array, rows, cols = region(p)
        way = pieces[p][1]
        return pltpu.make_async_remote_copy(
            src_ref=flow[array].at[step, rows, cols],
            dst_ref=flow[array].at[step + 1, rows, cols],
            send_sem=send_sem.at[p, step],
            recv_sem=recv_sem.at[p, step],
            device_id={"ctx": ring.right if way > 0 else ring.left},
            device_id_type=MESH,
        )

    def fetch(step):
        for p in range(len(pieces)):
            load(p, step).start()
            give(p, step).start()

    def add(p, step, first, last):
        array, _, row, rows, start, cols = pieces[p]
        width = 128 if cols % 128 == 0 else cols
        while width < 512 and cols % (2 * width) == 0:
            width *= 2
        rows = pl.ds(row, rows)

        def group(i, carry):
            at = start + i * width
            if cols > width:
                at = pl.multiple_of(at, 128)
            where = pl.ds(at, width)
            total = own[array][step, rows, where].astype(F32) + other[array][
                step, rows, where
            ].astype(F32)
            if not first:
                total += flow[array][step, rows, where].astype(F32)
            if last:
                outs[array][rows, where] = total.astype(outs[array].dtype)
            else:
                flow[array][step, rows, where] = total.astype(flow[array].dtype)
            return carry

        if cols == width:
            group(0, 0)
        else:
            lax.fori_loop(0, cols // width, group, 0)

    def work(step, first=False, last=False):
        for p in range(len(pieces)):
            load(p, step).wait()
            give(p, step).wait_recv()
            if not first:
                pass_on(p, step - 1).wait_recv()
            add(p, step, first, last)
            if not last:
                pass_on(p, step).start()

    for p in range(len(pieces)):
        load(p, 0).start()
    ring.enter()
    for p in range(len(pieces)):
        give(p, 0).start()
    for step in range(1, min(ahead, chips)):
        fetch(step)
    work(0, first=True)

    def middle(step, carry):
        @pl.when(step + ahead - 1 < chips)
        def _():
            fetch(step + ahead - 1)

        work(step)
        return carry

    lax.fori_loop(1, chips - 1, middle, 0)
    work(chips - 1, last=True)

    def drain(step, carry):
        for p in range(len(pieces)):
            give(p, step).wait_send()

            @pl.when(step < chips - 1)
            def _():
                pass_on(p, step).wait_send()

        return carry

    lax.fori_loop(0, chips, drain, 0)


def ring_sum(parts, pieces, devices, collective_id, ahead=3, name="ring_sum"):
    chips, count, arrays = devices // 2, len(pieces), len(parts)
    slots = [pltpu.VMEM((chips,) + p.shape[1:], p.dtype) for p in parts]
    return pl.pallas_call(
        functools.partial(ring_sum_kernel, devices, pieces, arrays, ahead),
        out_shape=[jax.ShapeDtypeStruct(p.shape[1:], F32) for p in parts],
        in_specs=[pl.BlockSpec(memory_space=pl.ANY)] * arrays,
        out_specs=[pl.BlockSpec(memory_space=pltpu.VMEM)] * arrays,
        scratch_shapes=slots * 3
        + [pltpu.SemaphoreType.DMA((count, chips))] * 3
        + [pltpu.SemaphoreType.DMA((count, chips - 1))] * 2,
        compiler_params=pltpu.CompilerParams(
            collective_id=collective_id, has_side_effects=True, vmem_limit_bytes=64000 * 1024
        ),
        name=name,
    )(*parts)


def split_ways(parts):
    pieces, lead = [], 1
    for i, p in enumerate(parts):
        _, rows, cols = p.shape
        tiles = cols // 128
        if cols % 128 == 0 and tiles > 1:
            left = (tiles + (1 if lead > 0 else 0)) // 2 * 128
            if tiles % 2:
                lead = -lead
            pieces.append((i, 1, 0, rows, 0, left))
            pieces.append((i, -1, 0, rows, left, cols - left))
        elif rows % 32 == 0:
            pieces.append((i, 1, 0, rows // 2, 0, cols))
            pieces.append((i, -1, rows // 2, rows // 2, 0, cols))
        else:
            pieces.append((i, 1, 0, rows, 0, cols))
    return tuple(pieces)


def sum_over_ctx(parts, pieces, devices, collective_id):
    if all(p.shape[1] % 8 == 0 for p in parts):
        return ring_sum(parts, pieces, devices, collective_id)
    return [
        lax.psum_scatter(p, "ctx", scatter_dimension=0, tiled=False).astype(F32) for p in parts
    ]


def front_kernel(
    devices,
    heads,
    tokens_ref,
    gains_ref,
    cos_ref,
    sin_ref,
    query_pos_ref,
    key_pos_ref,
    key_weight,
    value_weight,
    query_weight,
    out_weight,
    pairs_ref,
    normed_ref,
    key_ref,
    query_ref,
    query_low_ref,
    mixed_low_ref,
    mixed_ref,
    totals_ref,
    all_gains_ref,
    pair_whole,
    query_whole,
    out_whole,
    gains_other,
    own_sem,
    cross_send,
    cross_recv,
    side_send,
    side_recv,
    flow_send,
    flow_recv,
    twin_send,
    twin_recv,
):
    ring = Ring(devices)
    chips, far = ring.chips, ring.chips // 2
    me = lax.axis_index("ctx")
    mine = lax.axis_index("wsh")
    sequences, rows, width = tokens_ref.shape
    count = sequences * rows
    size = key_ref.shape[1]
    block = rows // 2
    stacked = heads * block
    weights = (key_weight, value_weight, query_weight, out_weight)

    def region(i, side, first, lines):
        if i == 3:
            start = side * out_weight.shape[0] + first
            return out_whole.at[pl.ds(pl.multiple_of(start, 16), lines)]
        cols = weights[i].shape[1]
        start = side * cols + (size if i == 1 else 0)
        target = query_whole if i == 2 else pair_whole
        return target.at[pl.ds(pl.multiple_of(first, 16), lines), pl.ds(pl.multiple_of(start, 128), cols)]

    def own(i):
        return pltpu.make_async_copy(
            weights[i], region(i, mine, 0, weights[i].shape[0]), own_sem.at[i]
        )

    def cross(i):
        if i == len(weights):
            source, target = gains_ref, gains_other
        else:
            half = weights[i].shape[0] // 2
            first = pl.multiple_of(ring.core * half, 16)
            source, target = weights[i].at[pl.ds(first, half)], region(i, mine, first, half)
        return pltpu.make_async_remote_copy(
            src_ref=source,
            dst_ref=target,
            send_sem=cross_send.at[i],
            recv_sem=cross_recv.at[i],
            device_id={"wsh": 1 - mine},
            device_id_type=MESH,
        )

    def side(i):
        half = weights[i].shape[0] // 2
        part = region(i, 1 - mine, ring.core * half, half)
        return pltpu.make_async_remote_copy(
            src_ref=part,
            dst_ref=part,
            send_sem=side_send.at[i],
            recv_sem=side_recv.at[i],
            device_id={"ctx": ring.partner},
            device_id_type=MESH,
        )

    def block_copy(way, seq, hop, target, send_sem, recv_sem):
        stream = (1 if way < 0 else 0) * sequences + seq
        place = (ring.place + chips - way * hop) % chips
        part = pairs_ref.at[ring.device(place, ring.core), seq]
        return pltpu.make_async_remote_copy(
            src_ref=part,
            dst_ref=part,
            send_sem=send_sem.at[stream, hop],
            recv_sem=recv_sem.at[stream, hop],
            device_id={"ctx": target},
            device_id_type=MESH,
        )

    def flow(way, seq, hop):
        target = ring.right if way > 0 else ring.left
        return block_copy(way, seq, hop, target, flow_send, flow_recv)

    def twin(way, seq, hop):
        return block_copy(way, seq, hop, ring.partner, twin_send, twin_recv)

    def hops(way, seq):
        return far if (seq % 2 == 0) == (way > 0) else far - 1

    streams = [(way, seq) for seq in range(sequences) for way in (1, -1)]

    def pass_on(hop):
        for way, seq in streams:
            if hop > hops(way, seq):
                continue
            if hop > 0:
                flow(way, seq, hop - 1).wait_recv()
            if hop < hops(way, seq):
                flow(way, seq, hop).start()
            if hop > 0 or way > 0:
                twin(way, seq, hop).start()

    def turned(value, gain):
        scale = lax.rsqrt(jnp.mean(value * value, -1, keepdims=True) + EPS)
        value = value * scale * gain
        first, second = value[:, : size // 2], value[:, size // 2 :]
        cosine, sine = cos_ref[...], sin_ref[...]
        return jnp.concatenate(
            [first * cosine - second * sine, second * cosine + first * sine], -1
        ).astype(BF16)

    def queries():
        gain = all_gains_ref[4:5, :size]
        for h in range(heads):
            cols = slice(h * size, (h + 1) * size)
            value = dot(normed_ref[...], query_whole[:, cols], ((1,), (0,)))
            query_ref[:, cols] = value
            query_low_ref[:, :, cols] = turned(value, gain).reshape(sequences, rows, size)

    def attention(seq, carry):
        chunk = min(devices, 16)
        asked, sums, totals = [], [], []
        for half in range(2):
            lines = slice(half * block, (half + 1) * block)
            asked.append(
                jnp.concatenate(
                    [query_low_ref[seq, lines, h * size : (h + 1) * size] for h in range(heads)], 0
                )
            )
            sums.append(jnp.zeros((stacked, size), F32))
            totals.append(jnp.zeros((stacked, 1), F32))
        for first in range(0, devices, chunk):
            span = slice(first * block, (first + chunk) * block)
            for key_half in range(2):
                part = pairs_ref[
                    first : first + chunk, seq, key_half * block : (key_half + 1) * block, :
                ].reshape(chunk * block, 2 * size)
                keys, values = part[:, :size], part[:, size:]
                for half in range(key_half, 2):
                    weights = jnp.exp(dot(asked[half], keys, ((1,), (1,))) * SCORE_SCALE)
                    if half == key_half:
                        allowed = (
                            key_pos_ref[key_half : key_half + 1, span]
                            <= query_pos_ref[half * stacked : (half + 1) * stacked, :]
                        )
                        weights = jnp.where(allowed, weights, 0.0)
                    low = weights.astype(BF16)
                    totals[half] += jnp.sum(low.astype(F32), -1, keepdims=True)
                    sums[half] += dot(low, values, ((1,), (0,)))
        for half in range(2):
            mixed = sums[half] / totals[half]
            span = slice(half * stacked, (half + 1) * stacked)
            mixed_ref[seq, span, :] = mixed
            totals_ref[seq, span, :] = jnp.broadcast_to(
                totals[half], (stacked, totals_ref.shape[2])
            )
            for h in range(heads):
                mixed_low_ref[
                    seq, half * block : (half + 1) * block, h * size : (h + 1) * size
                ] = mixed[h * block : (h + 1) * block].astype(BF16)
        return carry

    for i in range(len(weights)):
        own(i).start()
    ring.enter(across=True)
    order = (len(weights), 0, 1, 2, 3)
    for i in order:
        cross(i).start()
    inputs = tokens_ref[...].reshape(count, width).astype(F32)
    scale = lax.rsqrt(jnp.mean(inputs * inputs, -1, keepdims=True) + EPS)
    cross(len(weights)).wait_recv()
    all_gains_ref[...] = gains_ref[...] + gains_other[...]
    normed_ref[...] = (inputs * scale * all_gains_ref[0:1, :]).astype(BF16)
    for i in (0, 1):
        cross(i).wait_recv()
        side(i).start()
    for i in (0, 1):
        own(i).wait()
        side(i).wait_recv()
    value = dot(normed_ref[...], pair_whole[...], ((1,), (0,)))
    key_ref[...] = value[:, :size]
    key_low = turned(value[:, :size], all_gains_ref[4:5, size : 2 * size])
    pairs_ref[me, :, :, :size] = key_low.reshape(sequences, rows, size)
    pairs_ref[me, :, :, size:] = value[:, size:].astype(BF16).reshape(sequences, rows, size)
    pass_on(0)
    pass_on(1)
    cross(2).wait_recv()
    side(2).start()
    for hop in range(2, far + 1):
        pass_on(hop)
        if hop == 2:
            own(2).wait()
            side(2).wait_recv()
            queries()
    cross(3).wait_recv()
    side(3).start()
    for hop in range(far + 1):
        for way, seq in streams:
            if hop <= hops(way, seq) and (hop > 0 or way > 0):
                twin(way, seq, hop).wait_recv()
    lax.fori_loop(0, sequences, attention, 0)
    for hop in range(far + 1):
        for way, seq in streams:
            if hop > hops(way, seq):
                continue
            if hop > 0 or way > 0:
                twin(way, seq, hop).wait_send()
            if hop < hops(way, seq):
                flow(way, seq, hop).wait_send()
    own(3).wait()
    side(3).wait_recv()
    for i in order:
        cross(i).wait_send()
    for i in range(len(weights)):
        side(i).wait_send()


def front(tokens, gains, cosine, sine, query_pos, key_pos, weights, heads, devices, collective_id):
    sequences, rows, width = tokens.shape
    size = 2 * cosine.shape[1]
    count = sequences * rows
    far = devices // 4
    stacked = query_pos.shape[0]
    here, there = pl.BlockSpec(memory_space=pltpu.VMEM), pl.BlockSpec(memory_space=pl.ANY)
    streams = pltpu.SemaphoreType.DMA((2 * sequences, far + 1))
    outs = [
        ((devices, sequences, rows, 2 * size), BF16),
        ((count, width), BF16),
        ((count, size), F32),
        ((count, heads * size), F32),
        ((sequences, rows, heads * size), BF16),
        ((sequences, rows, heads * size), BF16),
        ((sequences, stacked, size), F32),
        ((sequences, stacked, 128), F32),
        (gains.shape, F32),
        ((width, 2 * size), BF16),
        ((width, heads * size), BF16),
        ((width, heads * size), BF16),
    ]
    return pl.pallas_call(
        functools.partial(front_kernel, devices, heads),
        in_specs=[here] * 6 + [there] * 4,
        out_specs=[here] * len(outs),
        out_shape=[jax.ShapeDtypeStruct(shape, kind) for shape, kind in outs],
        scratch_shapes=[pltpu.VMEM(gains.shape, gains.dtype)]
        + [pltpu.SemaphoreType.DMA((4,))]
        + [pltpu.SemaphoreType.DMA((5,))] * 2
        + [pltpu.SemaphoreType.DMA((4,))] * 2
        + [streams] * 4,
        compiler_params=pltpu.CompilerParams(
            collective_id=collective_id, has_side_effects=True, vmem_limit_bytes=67043328
        ),
        name="front",
    )(tokens, gains, cosine, sine, query_pos, key_pos, *weights)


class RingSum:
    def __init__(self, ring, pieces, parts, own, other, flow, outs, sems):
        self.ring, self.pieces, self.parts, self.own = ring, pieces, parts, own
        self.other, self.flow, self.outs = other, flow, outs
        self.put_sem, self.got_sem, self.send_sem, self.recv_sem = sems[:4]
        self.own_sem = sems[4] if own is not None else None
        self.last = ring.chips - 1

    def region(self, p):
        array, _, first, rows, start, cols = self.pieces[p]
        return array, pl.ds(first, rows), pl.ds(start, cols)

    def owner(self, p, step, core):
        way = self.pieces[p][1]
        chips = self.ring.chips
        return self.ring.device((self.ring.place + 2 * chips + way * (-1 - step)) % chips, core)

    def load(self, p, step):
        array, rows, cols = self.region(p)
        slot = step % self.own[array].shape[0]
        return pltpu.make_async_copy(
            self.parts[array].at[self.owner(p, step, self.ring.core), rows, cols],
            self.own[array].at[slot, rows, cols],
            self.own_sem.at[p, step],
        )

    def give(self, p, step):
        array, rows, cols = self.region(p)
        return pltpu.make_async_remote_copy(
            src_ref=self.parts[array].at[self.owner(p, step, 1 - self.ring.core), rows, cols],
            dst_ref=self.other[array].at[step, rows, cols],
            send_sem=self.put_sem.at[p, step],
            recv_sem=self.got_sem.at[p, step],
            device_id={"ctx": self.ring.partner},
            device_id_type=MESH,
        )

    def hop(self, p, step):
        array, rows, cols = self.region(p)
        way = self.pieces[p][1]
        return pltpu.make_async_remote_copy(
            src_ref=self.flow[array].at[step, rows, cols],
            dst_ref=self.flow[array].at[step + 1, rows, cols],
            send_sem=self.send_sem.at[p, step],
            recv_sem=self.recv_sem.at[p, step],
            device_id={"ctx": self.ring.right if way > 0 else self.ring.left},
            device_id_type=MESH,
        )

    def load_all(self, step):
        for p in range(len(self.pieces)):
            self.load(p, step).start()

    def give_all(self, step):
        for p in range(len(self.pieces)):
            self.give(p, step).start()

    def work(self, p, step):
        array, _, row, rows, start, cols = self.pieces[p]
        if self.own is not None:
            self.load(p, step).wait()
            mine, at_mine = self.own[array], step % self.own[array].shape[0]
        else:
            mine, at_mine = self.parts[array], self.owner(p, step, self.ring.core)
        self.give(p, step).wait_recv()
        if step > 0:
            self.hop(p, step - 1).wait_recv()
        width = 128 if cols % 128 == 0 else cols
        while width < 512 and cols % (2 * width) == 0:
            width *= 2
        rows = pl.ds(row, rows)

        def group(i, carry):
            at = start + i * width
            if cols > width:
                at = pl.multiple_of(at, 128)
            where = pl.ds(at, width)
            total = mine[at_mine, rows, where].astype(F32)
            total += self.other[array][step, rows, where].astype(F32)
            if step > 0:
                total += self.flow[array][step, rows, where].astype(F32)
            if step == self.last:
                self.outs[array][rows, where] = total.astype(self.outs[array].dtype)
            else:
                self.flow[array][step, rows, where] = total.astype(self.flow[array].dtype)
            return carry

        if cols == width:
            group(0, 0)
        else:
            lax.fori_loop(0, cols // width, group, 0)
        if step < self.last:
            self.hop(p, step).start()

    def drain(self):
        for p in range(len(self.pieces)):
            for step in range(self.last + 1):
                self.give(p, step).wait_send()
                if step < self.last:
                    self.hop(p, step).wait_send()


def norm_back(upstream, vector, gain):
    scale = lax.rsqrt(jnp.mean(vector * vector, -1, keepdims=True) + EPS)
    normal = vector * scale
    weighted = upstream * gain
    back = scale * (weighted - normal * jnp.mean(weighted * normal, -1, keepdims=True))
    return back, jnp.sum(upstream * normal, 0, keepdims=True)


GELU_SCALE = math.sqrt(2.0 / math.pi)
GELU_CUBE = 0.044715


def feed_forward_kernel(
    mixed_ref,
    tokens_ref,
    cotangent_ref,
    gains_ref,
    out_hbm,
    gate_hbm,
    up_hbm,
    down_hbm,
    output_ref,
    hidden_back_ref,
    mixed_back_ref,
    attended_own_ref,
    attended_send_ref,
    gain_part_ref,
    down_grad_hbm,
    gate_grad_hbm,
    up_grad_hbm,
    gate_weight,
    up_weight,
    down_weight,
    out_weight,
    attended_ref,
    ff_rows,
    low_rows,
    ff_turned,
    low_turned,
    gate,
    upward,
    activated,
    partial,
    part_send,
    part_recv,
    back_send,
    back_recv,
    hidden_ref,
    staging,
    load_sem,
    out_sem,
    store_sem,
    cross_send,
    cross_recv,
):
    count, width = attended_ref.shape
    hidden_units = gate_weight.shape[1]
    block = part_send.shape[0] // 2
    chunk = staging.shape[2]
    whole_chunks = hidden_units // chunk
    rest = hidden_units - whole_chunks * chunk
    mine = lax.axis_index("wsh")
    weights = ((gate_hbm, gate_weight), (up_hbm, up_weight), (down_hbm, down_weight))

    def load(w, at, size, index):
        source, target = weights[w]
        cols = pl.ds(at, size)
        return pltpu.make_async_copy(source.at[:, cols], target.at[:, cols], load_sem.at[w, index])

    def chunks(work):
        def step(c, carry):
            work(pl.multiple_of(c * chunk, 128), chunk, c)
            return carry

        lax.fori_loop(0, whole_chunks, step, 0)
        if rest:
            work(whole_chunks * chunk, rest, whole_chunks)

    def across(kind, piece, source, target):
        return pltpu.make_async_remote_copy(
            src_ref=source,
            dst_ref=target,
            send_sem=cross_send.at[kind, piece],
            recv_sem=cross_recv.at[kind, piece],
            device_id={"wsh": 1 - mine},
            device_id_type=MESH,
        )

    def swap_rows(kind, ref, piece):
        first = pl.multiple_of(piece * block, block)
        return across(
            kind, piece, ref.at[pl.ds(first, block)], ref.at[pl.ds(count + first, block)]
        )

    def swap_parts(kind, source, target, piece):
        lines = pl.ds(pl.multiple_of(piece * block, block), block)
        return across(kind, piece, source.at[lines], target.at[lines])

    def start_load(at, size, index):
        for w in range(3):
            load(w, at, size, index).start()

    bring_out = pltpu.make_async_copy(out_hbm, out_weight, out_sem.at[0])
    bring_out.start()
    chunks(start_load)
    barrier = pltpu.get_barrier_semaphore()
    pl.semaphore_signal(barrier, inc=1, device_id={"wsh": 1 - mine}, device_id_type=MESH)

    bring_out.wait()
    attended = dot(mixed_ref[...], out_weight[...], ((1,), (1,)))
    attended_ref[...] = attended
    scale = lax.rsqrt(jnp.mean(attended * attended, -1, keepdims=True) + EPS)
    hidden = tokens_ref[...].astype(F32) + attended * scale * gains_ref[1:2, :]
    hidden_ref[...] = hidden
    scale = lax.rsqrt(jnp.mean(hidden * hidden, -1, keepdims=True) + EPS)
    ff_rows[:count, :] = (hidden * scale * gains_ref[2:3, :]).astype(BF16)
    pl.semaphore_wait(barrier, 1)
    for piece in range(2):
        swap_rows(0, ff_rows, piece).start()

    def forward(turn, carry):
        b = (2 * turn) % 5 - (2 * turn) % 5 // 4

        @pl.when(b >= 2)
        def _():
            swap_rows(0, ff_rows, b - 2).wait_recv()

        lines = pl.ds(pl.multiple_of(b * block, block), block)

        def columns(at, size, index):
            @pl.when(b == 0)
            def _():
                for w in range(3):
                    load(w, at, size, index).wait()

            cols = pl.ds(at, size)
            g = dot(ff_rows[lines, :], gate_weight[:, cols], ((1,), (0,)))
            u = dot(ff_rows[lines, :], up_weight[:, cols], ((1,), (0,)))
            t = jnp.tanh(GELU_SCALE * (g + GELU_CUBE * g * g * g))
            gate[lines, cols] = g.astype(BF16)
            upward[lines, cols] = u.astype(BF16)
            activated[lines, cols] = (0.5 * g * (1.0 + t) * u).astype(BF16)

        chunks(columns)
        value = dot(activated[lines, :], down_weight[...], ((1,), (1,)))

        @pl.when(b < 2)
        def _():
            partial[lines, :] = value

        @pl.when(b >= 2)
        def _():
            there = pl.ds(pl.multiple_of((b - 2) * block, block), block)
            part_send[there, :] = value.astype(BF16)
            swap_parts(1, part_send, part_recv, b - 2).start()

        return carry

    lax.fori_loop(0, 4, forward, 0)
    ff_turned[...] = ff_rows[...].T
    for piece in range(2):
        swap_parts(1, part_send, part_recv, piece).wait_recv()
    lowered = partial[...] + part_recv[...].astype(F32)
    cotangent = cotangent_ref[...].astype(F32)
    back, part = norm_back(cotangent, lowered, gains_ref[3:4, :])
    low_rows[:count, :] = back.astype(BF16)
    for piece in range(2):
        swap_rows(2, low_rows, piece).start()
    gain_part_ref[...] = jnp.zeros_like(gain_part_ref)
    gain_part_ref[3:4, :] = part
    scale = lax.rsqrt(jnp.mean(lowered * lowered, -1, keepdims=True) + EPS)
    output_ref[...] = (hidden_ref[...] + lowered * scale * gains_ref[3:4, :]).astype(BF16)

    def backward(turn, carry):
        b = (2 * turn) % 5 - (2 * turn) % 5 // 4

        @pl.when(b >= 2)
        def _():
            swap_rows(2, low_rows, b - 2).wait_recv()

        lines = pl.ds(pl.multiple_of(b * block, block), block)

        def columns(at, size, index):
            cols = pl.ds(at, size)
            d = dot(low_rows[lines, :], down_weight[:, cols], ((1,), (0,)))
            g = gate[lines, cols].astype(F32)
            u = upward[lines, cols].astype(F32)
            square = g * g
            t = jnp.tanh(GELU_SCALE * (g + GELU_CUBE * square * g))
            half = 0.5 * (1.0 + t)
            slope = half + 0.5 * g * (1.0 - t * t) * (
                GELU_SCALE * (1.0 + 3.0 * GELU_CUBE * square)
            )
            gate[lines, cols] = (d * u * slope).astype(BF16)
            upward[lines, cols] = (d * g * half).astype(BF16)

        chunks(columns)
        value = dot(gate[lines, :], gate_weight[...], ((1,), (1,)))
        value += dot(upward[lines, :], up_weight[...], ((1,), (1,)))

        @pl.when(b < 2)
        def _():
            partial[lines, :] = value

        @pl.when(b >= 2)
        def _():
            there = pl.ds(pl.multiple_of((b - 2) * block, block), block)
            back_send[there, :] = value.astype(BF16)
            swap_parts(3, back_send, back_recv, b - 2).start()

        return carry

    lax.fori_loop(0, 4, backward, 0)
    low_turned[...] = low_rows[...].T

    grads = (
        (low_turned, activated, down_grad_hbm),
        (ff_turned, gate, gate_grad_hbm),
        (ff_turned, upward, up_grad_hbm),
    )

    def store(m, at, size, index):
        cols = pl.ds(at, size)
        return pltpu.make_async_copy(
            staging.at[index % 2, :, pl.ds(0, size)], grads[m][2].at[:, cols], store_sem.at[m, index]
        )

    for m in range(3):
        left, right, _ = grads[m]

        def columns(at, size, index, m=m, left=left, right=right):
            @pl.when(index >= 2)
            def _():
                store(m, 0, chunk, index - 2).wait()

            for top in range(0, width, width // 2):
                lines = slice(top, top + width // 2)
                staging[index % 2, lines, :size] = dot(
                    left[lines, :], right[:, pl.ds(at, size)], ((1,), (0,))
                ).astype(BF16)
            store(m, at, size, index).start()

        chunks(columns)
        last = whole_chunks + (1 if rest else 0)
        for index in range(max(last - 2, 0), last):
            store(m, 0, rest if index == whole_chunks else chunk, index).wait()

    for piece in range(2):
        swap_parts(3, back_send, back_recv, piece).wait_recv()
    upstream = partial[...] + back_recv[...].astype(F32)
    back, part = norm_back(upstream, hidden_ref[...], gains_ref[2:3, :])
    gain_part_ref[2:3, :] = part
    back += cotangent_ref[...].astype(F32)
    hidden_back_ref[...] = back
    back, part = norm_back(back, attended_ref[...], gains_ref[1:2, :])
    gain_part_ref[1:2, :] = part
    mixed_back_ref[...] = dot(back.astype(BF16), out_weight[...], ((1,), (0,))).astype(BF16)
    first, second = back[:, : width // 2].astype(BF16), back[:, width // 2 :].astype(BF16)
    attended_own_ref[...] = jnp.where(mine == 0, first, second)
    attended_send_ref[...] = jnp.where(mine == 0, second, first)
    for piece in range(2):
        swap_rows(0, ff_rows, piece).wait_send()
        swap_parts(1, part_send, part_recv, piece).wait_send()
        swap_rows(2, low_rows, piece).wait_send()
        swap_parts(3, back_send, back_recv, piece).wait_send()


def feed_forward(mixed, tokens, cotangent, gains, weights, collective_id):
    count, width = tokens.shape
    hidden_units = weights[1].shape[1]
    chunk = 512
    pieces = -(-hidden_units // chunk)
    here, there = pl.BlockSpec(memory_space=pltpu.VMEM), pl.BlockSpec(memory_space=pl.ANY)
    like = lambda shape, kind: jax.ShapeDtypeStruct(shape, kind)
    matrix = (width, hidden_units)
    return pl.pallas_call(
        feed_forward_kernel,
        in_specs=[here] * 4 + [there] * 4,
        out_specs=[here] * 6 + [there] * 3,
        out_shape=[
            like((count, width), BF16),
            like((count, width), F32),
            like(mixed.shape, BF16),
            like((count, width // 2), BF16),
            like((count, width // 2), BF16),
            like(gains.shape, F32),
        ]
        + [like(matrix, BF16)] * 3,
        scratch_shapes=[pltpu.VMEM(matrix, BF16)] * 3
        + [pltpu.VMEM(weights[0].shape, BF16), pltpu.VMEM((count, width), F32)]
        + [pltpu.VMEM((2 * count, width), BF16)] * 2
        + [pltpu.VMEM((width, 2 * count), BF16)] * 2
        + [pltpu.VMEM((2 * count, hidden_units), BF16)] * 3
        + [pltpu.VMEM((count, width), F32)]
        + [pltpu.VMEM((count, width), BF16)] * 4
        + [
            pltpu.VMEM((count, width), F32),
            pltpu.VMEM((2, width, chunk), BF16),
            pltpu.SemaphoreType.DMA((3, pieces)),
            pltpu.SemaphoreType.DMA((1,)),
            pltpu.SemaphoreType.DMA((3, pieces)),
            pltpu.SemaphoreType.DMA((4, 2)),
            pltpu.SemaphoreType.DMA((4, 2)),
        ],
        compiler_params=pltpu.CompilerParams(
            collective_id=collective_id, has_side_effects=True, vmem_limit_bytes=67043328
        ),
        name="feed_forward",
    )(mixed, tokens, cotangent, gains, *weights)


def turn_back(upstream, cosine, sine):
    middle = upstream.shape[-1] // 2
    first, second = upstream[:, :middle], upstream[:, middle:]
    return jnp.concatenate([first * cosine + second * sine, second * cosine - first * sine], -1)


def back_kernel(devices, heads, ff_pieces, kv_pieces, attn_pieces, names, *refs):
    r = dict(zip(names, refs))
    ring = Ring(devices)
    chips = ring.chips
    mine = lax.axis_index("wsh")
    sequences, rows, _ = r["query"].shape
    size = r["key_raw"].shape[1]
    count = sequences * rows
    block = rows // 2
    stacked = heads * block

    ff = RingSum(
        ring,
        ff_pieces,
        [r["part_down"], r["part_gate"], r["part_up"]],
        [r[f"ff_own{i}"] for i in range(3)],
        [r[f"ff_other{i}"] for i in range(3)],
        [r[f"ff_flow{i}"] for i in range(3)],
        [r["grad_down"], r["grad_gate"], r["grad_up"]],
        [r["ff_put"], r["ff_got"], r["ff_send"], r["ff_recv"], r["ff_load"]],
    )
    kv = RingSum(
        ring,
        kv_pieces,
        [r["pairs"]],
        None,
        [r["kv_other"]],
        [r["kv_flow"]],
        [r["kv_sum"]],
        [r["kv_put"], r["kv_got"], r["kv_send"], r["kv_recv"]],
    )
    attn = RingSum(
        ring,
        attn_pieces,
        [r["qkv_part"], r["out_part"]],
        None,
        [r["qkv_other"], r["out_other"]],
        [r["qkv_flow"], r["out_flow"]],
        [r["grad_qkv"], r["grad_out"]],
        [r["at_put"], r["at_got"], r["at_send"], r["at_recv"]],
    )

    def brought(i):
        name = BROUGHT[i]
        return pltpu.make_async_copy(r["in_" + name], r[name], r["bring"].at[i])

    def need(*wanted):
        for name in wanted:
            brought(BROUGHT.index(name)).wait()

    def across(i, source, target):
        return pltpu.make_async_remote_copy(
            src_ref=source,
            dst_ref=target,
            send_sem=r["cross_send"].at[i],
            recv_sem=r["cross_recv"].at[i],
            device_id={"wsh": 1 - mine},
            device_id_type=MESH,
        )

    out_swap = across(0, r["att_send"], r["att_across"])
    col_swap = across(1, r["col_send"], r["col_rows"].at[pl.ds(count, count)])
    gain_swap = across(2, r["gain_own"], r["gain_across"])
    gain_twin = pltpu.make_async_remote_copy(
        src_ref=r["gain_pair"],
        dst_ref=r["gain_twin"],
        send_sem=r["twin_send"].at[0],
        recv_sem=r["twin_recv"].at[0],
        device_id={"ctx": ring.partner},
        device_id_type=MESH,
    )

    def gain_hop(way, step):
        return pltpu.make_async_remote_copy(
            src_ref=r["gain_flow"].at[way, step],
            dst_ref=r["gain_flow"].at[way, step + 1],
            send_sem=r["gain_send"].at[way, step],
            recv_sem=r["gain_recv"].at[way, step],
            device_id={"ctx": ring.right if way == 0 else ring.left},
            device_id_type=MESH,
        )

    gain_hops = (chips // 2, chips - 1 - chips // 2)

    def attention(seq, carry):
        queries, scaled, correction = [], [], []
        for half in range(2):
            span = slice(half * stacked, (half + 1) * stacked)
            lines = slice(half * block, (half + 1) * block)
            cut = lambda ref: jnp.concatenate(
                [ref[seq, lines, h * size : (h + 1) * size] for h in range(heads)], 0
            )
            queries.append(cut(r["query"]))
            grad = cut(r["grad_mixed"]).astype(F32)
            total = r["totals"][seq, span, :1]
            delta = jnp.sum(grad * r["mixed"][seq, span, :], -1, keepdims=True)
            scaled.append((grad / total).astype(BF16))
            correction.append(delta / total)
        grad_query = [jnp.zeros((stacked, size), F32) for _ in range(2)]
        for key_half in range(2):
            lines = pl.ds(pl.multiple_of(seq * rows + key_half * block, block), block)
            part = r["pairs"][:, lines, :].reshape(devices * block, 2 * size)
            keys, values = part[:, :size], part[:, size:]
            grad_keys = jnp.zeros((devices * block, size), F32)
            grad_values = jnp.zeros((devices * block, size), F32)
            for half in range(key_half, 2):
                weights = jnp.exp(dot(queries[half], keys, ((1,), (1,))) * SCORE_SCALE)
                if half == key_half:
                    allowed = (
                        r["key_pos"][key_half : key_half + 1, :]
                        <= r["query_pos"][half * stacked : (half + 1) * stacked, :]
                    )
                    weights = jnp.where(allowed, weights, 0.0)
                low = weights.astype(BF16)
                grad_weights = dot(scaled[half], values, ((1,), (1,)))
                grad_scores = (weights * (grad_weights - correction[half])).astype(BF16)
                grad_query[half] += dot(grad_scores, keys, ((1,), (0,)))
                grad_keys += dot(grad_scores, queries[half], ((0,), (0,)))
                grad_values += dot(low, scaled[half], ((0,), (0,)))
            both = jnp.concatenate([grad_keys * SCORE_SCALE, grad_values], -1).astype(BF16)
            r["pairs"][:, lines, :] = both.reshape(devices, block, 2 * size)
        for half in range(2):
            r["mixed"][seq, half * stacked : (half + 1) * stacked, :] = grad_query[half] * SCORE_SCALE
        return carry

    def pick(value, which):
        middle = value.shape[1] // 2
        return jnp.where(which == 0, value[:, :middle], value[:, middle:])

    def projections():
        need("query_raw", "key_raw", "cosine", "sine", "gains")
        cosine, sine = r["cosine"][...], r["sine"][...]
        gain = r["gains"][4:5, :size]
        total = jnp.zeros((1, size), F32)
        lows = []
        for h in range(heads):
            cols = slice(h * size, (h + 1) * size)
            grad = jnp.concatenate(
                [
                    r["mixed"][seq, half * stacked + h * block : half * stacked + (h + 1) * block, :]
                    for seq in range(sequences)
                    for half in range(2)
                ],
                0,
            )
            back, part = norm_back(
                turn_back(grad, cosine, sine), r["query_raw"][:, cols], gain
            )
            total += part
            r["query_low"][:, cols] = back.astype(BF16)
        back, key_total = norm_back(
            turn_back(r["kv_sum"][:, :size], cosine, sine),
            r["key_raw"][...],
            r["gains"][4:5, size : 2 * size],
        )
        r["pair_low"][:, :size] = back.astype(BF16)
        r["pair_low"][:, size:] = r["kv_sum"][:, size:].astype(BF16)
        first = 0
        for value in (
            r["query_low"][...],
            r["pair_low"][:, :size],
            r["pair_low"][:, size:],
        ):
            cols = slice(first, first + value.shape[1] // 2)
            r["col_rows"][:count, cols] = pick(value, mine)
            r["col_send"][:, cols] = pick(value, 1 - mine)
            first += value.shape[1] // 2
        col_swap.start()
        need("weight_query", "weight_pair", "tokens", "grad_hidden", "gain_part")
        grad_normed = dot(r["query_low"][...], r["weight_query"][...], ((1,), (1,)))
        grad_normed += dot(r["pair_low"][...], r["weight_pair"][...], ((1,), (1,)))
        back, part = norm_back(grad_normed, r["tokens"][...].astype(F32), r["gains"][0:1, :])
        r["grad_tokens"][...] = back + r["grad_hidden"][...]
        r["gain_own"][...] = r["gain_part"][...]
        r["gain_own"][0:1, :] = part
        r["gain_own"][4:5, :size] = total
        r["gain_own"][4:5, size : 2 * size] = key_total
        gain_swap.start()

    def out_part():
        need("mixed_own", "mixed_other", "att_own")
        out_swap.wait_recv()
        _, lines, cols = r["out_part"].shape
        value = dot(r["mixed_own"][...], r["att_own"][...], ((0,), (0,)))
        value += dot(r["mixed_other"][...], r["att_across"][...], ((0,), (0,)))
        r["out_part"][...] = value.reshape(devices, lines, cols).astype(BF16)

    def turn_rows():
        need("normed_own", "normed_other")
        r["weight_pair"][:, :count] = r["normed_own"][...].T
        r["weight_pair"][:, count:] = r["normed_other"][...].T

    def qkv_part():
        col_swap.wait_recv()
        _, lines, cols = r["qkv_part"].shape
        width = 256
        for first in range(0, cols, width):
            value = dot(
                r["weight_pair"][...], r["col_rows"][:, first : first + width], ((1,), (0,))
            )
            r["qkv_part"][:, :, first : first + width] = value.reshape(
                devices, lines, width
            ).astype(BF16)

    def gains_step(step):
        if step == 0:
            gain_swap.wait_recv()
            r["gain_pair"][...] = r["gain_own"][...] + r["gain_across"][...]
            gain_twin.start()
        elif step == 1:
            gain_twin.wait_recv()
            both = r["gain_pair"][...] + r["gain_twin"][...]
            r["gain_flow"][0, 0] = both
            r["gain_flow"][1, 0] = both
            r["gain_sum"][...] = both
            for way in range(2):
                gain_hop(way, 0).start()
        else:
            for way in range(2):
                if step - 2 < gain_hops[way]:
                    gain_hop(way, step - 2).wait_recv()
                    if step - 1 < gain_hops[way]:
                        gain_hop(way, step - 1).start()
                    r["gain_sum"][...] += r["gain_flow"][way, step - 1]

    def ff_step(step, extra=()):
        extra = list(extra)
        if step + 1 < chips:
            ff.load_all(step + 1)
        if step + 2 < chips:
            ff.give_all(step + 2)
        for p in range(len(ff_pieces)):
            ff.work(p, step)
            if p % 2 == 1 and extra:
                extra.pop(0)()
        for left in extra:
            left()

    def kv_step(step):
        def run():
            for p in range(len(kv_pieces)):
                kv.work(p, step)

        return run

    def attn_step(step):
        def run():
            gains_step(step)
            for p in range(len(attn_pieces)):
                attn.work(p, step)

        return run

    ff.load_all(0)
    for i in range(len(BROUGHT)):
        brought(i).start()
    ring.enter(across=True)
    ff.give_all(0)
    ff.give_all(1)
    need("att_send")
    out_swap.start()
    ff_step(0)
    need("pairs", "query", "grad_mixed", "mixed", "totals", "query_pos", "key_pos")
    lax.fori_loop(0, sequences, attention, 0)
    for step in range(chips):
        kv.give_all(step)
    ff_step(1, [kv_step(0), kv_step(1), kv_step(2)])
    ff_step(2, [kv_step(3), kv_step(4), kv_step(5)])
    ff_step(3, [kv_step(6), kv_step(7), out_part])
    projections()
    ff_step(4, [turn_rows])
    qkv_part()
    for step in range(chips):
        attn.give_all(step)
    ff_step(5, [attn_step(0), attn_step(1), attn_step(2)])
    ff_step(6, [attn_step(3), attn_step(4), attn_step(5)])
    ff_step(7, [attn_step(6), attn_step(7)])
    r["gains_total"][...] = r["gain_sum"][...]
    for copy in (out_swap, col_swap, gain_swap, gain_twin):
        copy.wait_send()
    for way in range(2):
        for step in range(gain_hops[way]):
            gain_hop(way, step).wait_send()
    ff.drain()
    kv.drain()
    attn.drain()


BROUGHT = (
    "att_send",
    "pairs",
    "query",
    "grad_mixed",
    "mixed",
    "totals",
    "query_pos",
    "key_pos",
    "att_own",
    "mixed_own",
    "mixed_other",
    "query_raw",
    "key_raw",
    "cosine",
    "sine",
    "gains",
    "weight_query",
    "weight_pair",
    "tokens",
    "grad_hidden",
    "gain_part",
    "normed_own",
    "normed_other",
)


def back(given, ff_parts, heads, devices, collective_id):
    chips = devices // 2
    count, width = given["tokens"].shape
    size = given["key_raw"].shape[1]
    out_cols = given["att_send"].shape[1]
    out_lines = given["mixed_own"].shape[1] // devices
    lines = width // devices
    cols = (heads * size + 2 * size) // 2
    slots = lambda n, p: pltpu.VMEM((n,) + tuple(p.shape[1:]), p.dtype)
    ff_pieces = split_ways(ff_parts)
    pair_rows = given["pairs"].shape[1]
    kv_pieces = tuple(
        (0, 1 - 2 * i, i * pair_rows // 2, pair_rows // 2, 0, 2 * size) for i in range(2)
    )
    attn_pieces = (
        (0, 1, 0, lines, 0, cols // 2),
        (0, -1, 0, lines, cols // 2, cols // 2),
        (1, 1, 0, out_lines // 2, 0, out_cols),
        (1, -1, out_lines // 2, out_lines // 2, 0, out_cols),
    )
    dma = lambda *shape: pltpu.SemaphoreType.DMA(shape)
    names, specs, operands = [], [], []
    for name, array in zip(("part_down", "part_gate", "part_up"), ff_parts):
        names.append(name)
        operands.append(array)
    for name in BROUGHT:
        names.append("in_" + name)
        operands.append(given[name])
    outs = {
        "grad_tokens": ((count, width), F32),
        "grad_down": (ff_parts[0].shape[1:], BF16),
        "grad_gate": (ff_parts[1].shape[1:], BF16),
        "grad_up": (ff_parts[2].shape[1:], BF16),
        "grad_qkv": ((lines, cols), F32),
        "grad_out": ((out_lines, out_cols), F32),
        "gains_total": (given["gains"].shape, F32),
    }
    scratch = {}
    for name in BROUGHT:
        shape = given[name].shape
        scratch[name] = pltpu.VMEM(shape, given[name].dtype)
    for i, p in enumerate(ff_parts):
        scratch[f"ff_own{i}"] = slots(2, p)
        scratch[f"ff_other{i}"] = slots(chips, p)
        scratch[f"ff_flow{i}"] = slots(chips, p)
    for kind, pieces in (("ff", ff_pieces), ("kv", kv_pieces), ("at", attn_pieces)):
        for name, steps in (("put", chips), ("got", chips), ("send", chips - 1), ("recv", chips - 1)):
            scratch[f"{kind}_{name}"] = dma(len(pieces), steps)
    scratch["ff_load"] = dma(len(ff_pieces), chips)
    scratch["kv_other"] = slots(chips, given["pairs"])
    scratch["kv_flow"] = slots(chips, given["pairs"])
    scratch["kv_sum"] = pltpu.VMEM((pair_rows, 2 * size), F32)
    scratch["att_across"] = pltpu.VMEM((count, out_cols), BF16)
    scratch["query_low"] = pltpu.VMEM((count, heads * size), BF16)
    scratch["pair_low"] = pltpu.VMEM((count, 2 * size), BF16)
    scratch["col_rows"] = pltpu.VMEM((2 * count, cols), BF16)
    scratch["col_send"] = pltpu.VMEM((count, cols), BF16)
    for name, shape in (("qkv", (lines, cols)), ("out", (out_lines, out_cols))):
        scratch[f"{name}_part"] = pltpu.VMEM((devices,) + shape, BF16)
        scratch[f"{name}_other"] = pltpu.VMEM((chips,) + shape, BF16)
        scratch[f"{name}_flow"] = pltpu.VMEM((chips,) + shape, BF16)
    for name in ("gain_own", "gain_across", "gain_pair", "gain_twin", "gain_sum"):
        scratch[name] = pltpu.VMEM(given["gains"].shape, F32)
    scratch["gain_flow"] = pltpu.VMEM((2, chips // 2 + 1) + given["gains"].shape, F32)
    scratch["bring"] = dma(len(BROUGHT))
    for name, n in (("cross_send", 3), ("cross_recv", 3), ("twin_send", 1), ("twin_recv", 1)):
        scratch[name] = dma(n)
    scratch["gain_send"] = dma(2, chips // 2)
    scratch["gain_recv"] = dma(2, chips // 2)
    names += list(outs) + list(scratch)
    return pl.pallas_call(
        functools.partial(
            back_kernel, devices, heads, ff_pieces, kv_pieces, attn_pieces, tuple(names)
        ),
        in_specs=[pl.BlockSpec(memory_space=pl.ANY)] * len(operands),
        out_specs=[pl.BlockSpec(memory_space=pltpu.VMEM)] * len(outs),
        out_shape=[jax.ShapeDtypeStruct(shape, kind) for shape, kind in outs.values()],
        scratch_shapes=list(scratch.values()),
        compiler_params=pltpu.CompilerParams(
            collective_id=collective_id, has_side_effects=True, vmem_limit_bytes=67043328
        ),
        name="back",
    )(*operands)


def body(
    tokens,
    block_order,
    gain_attn_pre,
    gain_query,
    gain_key,
    gain_attn_post,
    gain_ff_pre,
    gain_ff_post,
    weight_query,
    weight_key,
    weight_value,
    weight_out,
    weight_gate,
    weight_up,
    weight_down,
    cotangent,
):
    sequences, rows, width = tokens.shape
    count = sequences * rows
    block = rows // 2
    devices = lax.axis_size("ctx")
    me = lax.axis_index("ctx")
    mine = lax.axis_index("wsh")

    head_size = 2 * gain_key.shape[0]
    heads = 2 * weight_query.shape[1] // head_size

    lane = jnp.arange(block, dtype=jnp.int32)
    late_order = 2 * devices - 1 - block_order
    early_pos = (block_order[:, None] * block + lane[None]).reshape(-1)
    late_pos = (late_order[:, None] * block + lane[None]).reshape(-1)
    key_pos = jnp.stack([early_pos, late_pos], 0)
    own_first = lax.dynamic_slice_in_dim(block_order, me, 1)[0]
    own_early = own_first * block + lane
    own_late = (2 * devices - 1 - own_first) * block + lane
    own_pos = jnp.concatenate([own_early, own_late])
    query_pos = jnp.concatenate([jnp.tile(own_early, heads), jnp.tile(own_late, heads)])[:, None]

    cosine, sine = angle_tables(own_pos, head_size)

    def placed(gain):
        zeros = jnp.zeros_like(gain)
        return jnp.where(
            mine == 0, jnp.concatenate([gain, zeros]), jnp.concatenate([zeros, gain])
        ).astype(F32)

    own_gains = [placed(g) for g in (gain_attn_pre, gain_attn_post, gain_ff_pre, gain_ff_post)]
    small = [placed(gain_query), placed(gain_key)]
    own_gains.append(jnp.concatenate(small + [jnp.zeros((width - 2 * head_size,), F32)]))
    own_gains = jnp.stack(own_gains + [jnp.zeros((width,), F32)] * 3)
    (
        pairs,
        normed_rows,
        key_raw,
        query_raw,
        query_low,
        mixed_low,
        mixed,
        totals,
        all_gains,
        pair_weight,
        query_weight,
        out_weight,
    ) = front(
        tokens,
        own_gains,
        jnp.tile(cosine, (sequences, 1)),
        jnp.tile(sine, (sequences, 1)),
        query_pos,
        key_pos,
        (weight_key, weight_value, weight_query, weight_out.T),
        heads,
        devices,
        2,
    )
    attn_pre = all_gains[0]
    query_gain = all_gains[4, :head_size]
    key_gain = all_gains[4, head_size : 2 * head_size]
    mixed_rows = mixed_low.reshape(count, heads * head_size)
    local_size = weight_key.shape[1]
    inputs = tokens.astype(F32)

    def key_path(key_in, key_scale):
        return rotate(norm_gain(key_in, key_scale), cosine[None], sine[None])

    def query_path(query_in, query_scale):
        return rotate(
            norm_gain(query_in, query_scale), cosine[None, :, None, :], sine[None, :, None, :]
        )

    (
        output,
        grad_hidden,
        grad_mixed,
        attended_own,
        attended_send,
        gain_part,
        part_down,
        part_gate,
        part_up,
    ) = feed_forward(
        mixed_rows,
        tokens.reshape(count, width),
        cotangent.reshape(count, width),
        all_gains,
        (out_weight, weight_gate, weight_up, weight_down),
        3,
    )
    output = output.reshape(sequences, rows, width)

    def both(own, other):
        return jnp.concatenate([own, other], 0)

    def weight_grad(left, right):
        return dot(left, right, ((0,), (0,))).astype(BF16)

    grad_mixed = grad_mixed.reshape(query_low.shape)
    given = {
        "att_send": attended_send,
        "att_own": attended_own,
        "pairs": pairs.reshape(devices, count, 2 * head_size),
        "query": query_low,
        "grad_mixed": grad_mixed,
        "mixed": mixed,
        "totals": totals,
        "query_pos": query_pos,
        "key_pos": key_pos,
        "mixed_own": mixed_rows,
        "mixed_other": swap(mixed_rows),
        "query_raw": query_raw,
        "key_raw": key_raw,
        "cosine": jnp.tile(cosine, (sequences, 1)),
        "sine": jnp.tile(sine, (sequences, 1)),
        "gains": all_gains,
        "weight_query": query_weight,
        "weight_pair": pair_weight,
        "tokens": tokens.reshape(count, width),
        "grad_hidden": grad_hidden.reshape(count, width),
        "gain_part": gain_part,
        "normed_own": normed_rows,
        "normed_other": swap(normed_rows),
    }
    aligned = width % (8 * devices) == 0 and mixed_rows.shape[1] % (32 * devices) == 0
    if aligned and count == head_size:
        ff_parts = [
            p.reshape(devices, p.shape[0] // devices, p.shape[1])
            for p in (part_down, part_gate, part_up)
        ]
        grad_tokens, grad_down_w, grad_gate_w, grad_up_w, grad_qkv, grad_out_w, gain_sums = back(
            given, ff_parts, heads, devices, 0
        )
        grad_tokens = grad_tokens.reshape(sequences, rows, width)
        place = me * 2 + mine

        def share(row, first, size):
            part = size // (2 * devices)
            return lax.dynamic_slice(gain_sums, (row, first + place * part), (1, part))[0]

        outs = [
            share(0, 0, width),
            share(4, 0, head_size),
            share(4, head_size, head_size),
            share(1, 0, width),
            share(2, 0, width),
            share(3, 0, width),
        ]
    else:
        part_out = weight_grad(
            both(mixed_rows, swap(mixed_rows)),
            both(attended_own, swap(attended_send)),
        )
        grad_query, grad_pairs = attend_backward(
            query_low, pairs, grad_mixed, mixed, totals, query_pos, key_pos, heads
        )
        pair_rows = sequences * rows
        slots = grad_pairs.reshape(devices, pair_rows, 2 * head_size)
        share = pair_rows // 8
        pieces = tuple((0, 1 - 2 * (i % 2), i * share, share, 0, 2 * head_size) for i in range(8))
        own_grads = sum_over_ctx([slots], pieces, devices, 0)[0]
        own_grads = own_grads.reshape(sequences, rows, 2 * head_size)
        grad_key_raw, grad_key_gain = jax.vjp(
            key_path, key_raw.reshape(sequences, rows, head_size), key_gain
        )[1](own_grads[..., :head_size])
        value_grad_low = own_grads[..., head_size:].astype(BF16)
        grad_query_raw, grad_query_gain = jax.vjp(
            query_path, query_raw.reshape(sequences, rows, heads, head_size), query_gain
        )[1](
            grad_query.reshape(sequences, rows, heads, head_size)
        )
        query_grad_low = grad_query_raw.reshape(count, heads * head_size).astype(BF16)
        key_grad_low = grad_key_raw.astype(BF16).reshape(count, head_size)
        value_grad_low = value_grad_low.reshape(count, head_size)
        grad_normed = (
            dot(query_grad_low, query_weight, ((1,), (1,)))
            + dot(jnp.concatenate([key_grad_low, value_grad_low], -1), pair_weight, ((1,), (1,)))
        ).reshape(sequences, rows, width)
        grad_inputs, grad_attn_pre = jax.vjp(norm_gain, inputs, attn_pre)[1](grad_normed)
        grad_tokens = grad_inputs + grad_hidden.reshape(sequences, rows, width)

        def columns(which):
            return jnp.concatenate(
                [half_of(v, which) for v in (query_grad_low, key_grad_low, value_grad_low)], -1
            )

        part_qkv = weight_grad(
            both(normed_rows, swap(normed_rows)), both(columns(mine), swap(columns(1 - mine)))
        )

        gain_grads = [
            grad_attn_pre,
            grad_query_gain,
            grad_key_gain,
            gain_part[1],
            gain_part[2],
            gain_part[3],
        ]
        packed = jnp.concatenate([g.reshape(devices, 2, -1) for g in gain_grads], -1)
        keep = jnp.where(mine == 0, packed[:, 0], packed[:, 1])
        send = jnp.where(mine == 0, packed[:, 1], packed[:, 0])
        packed = keep + swap(send)
        gain_size = packed.shape[-1]
        packed = jnp.pad(packed, ((0, 0), (0, 1024 - gain_size))).reshape(devices, 8, 128)
        parts = [
            p.reshape(devices, p.shape[0] // devices, p.shape[1])
            for p in (part_down, part_gate, part_up, part_qkv, part_out)
        ] + [packed]
        grad_down_w, grad_gate_w, grad_up_w, grad_qkv, grad_out_w, packed = sum_over_ctx(
            parts, split_ways(parts), devices, 1
        )
        packed = packed.reshape(-1)
        outs, first = [], 0
        for g in gain_grads:
            size = g.shape[0] // (2 * devices)
            outs.append(packed[first : first + size])
            first += size
    query_cols = grad_qkv.shape[1] - 2 * local_size
    grad_query_w = grad_qkv[:, :query_cols]
    grad_key_w = grad_qkv[:, query_cols : query_cols + local_size]
    grad_value_w = grad_qkv[:, query_cols + local_size :]
    grad_down_w, grad_gate_w, grad_up_w = (
        g.astype(F32) for g in (grad_down_w, grad_gate_w, grad_up_w)
    )
    return (
        output,
        grad_tokens,
        *outs,
        grad_query_w,
        grad_key_w,
        grad_value_w,
        grad_out_w,
        grad_gate_w,
        grad_up_w,
        grad_down_w,
    )


def solution(mesh):
    rows, vector, matrix = P("wsh", "ctx", None), P("wsh"), P(None, "wsh")
    in_specs = (rows, P()) + (vector,) * 6 + (matrix,) * 7 + (rows,)
    out_specs = (rows, rows) + (P(("ctx", "wsh")),) * 6 + (P("ctx", "wsh"),) * 7
    return jax.shard_map(body, mesh=mesh, in_specs=in_specs, out_specs=out_specs, check_vma=False)
```

profile of v0, /device:TPU:0, one launch (start us, length us, event | category | flops | bytes accessed | tf_op | source)
XLA Modules:
  0.0 351.9 jit_solution(14570331936473966354)
XLA Ops:
  0.7 0.8 select_convert_fusion.2
  1.5 0.8 select_convert_fusion
  2.4 0.7 fusion.2
  3.2 0.7 broadcast_multiply_fusion
  3.8 1.2 dynamic_slice.21
  6.4 0.1 add_convert_fusion
  6.5 0.1 tile.23
  6.6 0.1 tile.21
  6.6 0.9 copy.31.query_pos_ref.refs_9_
  7.5 0.1 iota_add_fusion
  7.6 0.1 add.126
  7.7 0.1 add.122
  7.7 0.3 multiply_sine_fusion
  8.1 0.6 pad_add_fusion.key_pos_ref.refs_10_
  8.7 0.7 stack.46.gains_ref
  9.3 0.7 tile.16
  10.0 0.7 tile.18
  10.7 49.4 %front.1 = (bf16[16,2,128,512]{3,2,1,0:T(8,128)(2,1)}, bf16[256,1152]{1,0:T(8,128)(2,1)}, f32[256,256]{1,0:T(8,128)}, f32[256,1024]{1,0:T(8,128)}, bf16[2,128,10...) custom-call(bf16[2,128,1152]{2,1,0:T(8,128)(2,1)} %tokens_ref.1, ...), custom_call_target="tpu_custom_call" | custom-call | tf_op jit(solution)/shard_map/front/pallas_call | solution.py:596
  60.1 0.4 collective-permute-start.1
  60.5 1.7 collective-permute-start
  62.2 111.2 %feed_forward.1 = (bf16[256,1152]{1,0:T(8,128)(2,1)}, f32[256,1152]{1,0:T(8,128)}, bf16[256,1024]{1,0:T(8,128)(2,1)}, bf16[256,576]{1,0:T(8,128)(2,1)}, bf16[256...) custom-call(bf16[256,1024]{1,0:T(8,128)(2,1)} %bitcast.35, ...), custom_call_target="tpu_custom_call" | custom-call | tf_op jit(solution)/shard_map/feed_forward/pallas_call | solution.py:990
  173.4 164.9 %back.1 = (f32[256,1152]{1,0:T(8,128)}, bf16[72,3456]{1,0:T(8,128)(2,1)}, bf16[72,3456]{1,0:T(8,128)(2,1)}, bf16[72,3456]{1,0:T(8,128)(2,1)}, f32[72,768]{1,0:T(...) custom-call(bf16[16,72,3456]{2,1,0:T(8,128)(2,1)} %bitcast.28, bf16[16,72,3456]{2,1,0:T(8,128)(2,1)} %bitcast.29, ...), custom_call_target="tpu_custom_call" | custom-call | tf_op jit(solution)/shard_map/back/pallas_call | solution.py:1417
  338.3 1.6 slice.9
  340.0 1.5 fusion.4
  341.4 2.0 convert_element_type.29
  343.5 2.1 convert_element_type.30
  345.6 1.0 convert_element_type.31
  346.6 1.4 dynamic-slice_bitcast_fusion
  348.1 1.3 fusion.1
  349.4 0.8 copy.36
  350.2 1.0 copy.37
  351.2 0.7 copy.38
  (24 shorter events, 0.1 us)
Async XLA Ops:
  60.1 113.3 %collective-permute-start.1 = (bf16[256,1152]{1,0:T(8,128)(2,1)}, bf16[256,1152]{1,0:T(8,128)(2,1)}, u32[]{:S(2)}, u32[]{:S(2)}) collective-permute-start(bf16[256,1152]{1,0:T(8,128)(2,1)} %get-tuple-element.63.refs_24_), channel_id=1, source_target_pairs={{0,1},{1,0},{2,3},{3,2},{4,5},{5,4},{6,7},{7,6},{8,9},{9,8},{10,11... | collective-permute-start | bytes 1769480 | tf_op jit(solution)/shard_map/ppermute | solution.py:40
  60.5 112.9 %collective-permute-start = (bf16[256,1024]{1,0:T(8,128)(2,1)}, bf16[256,1024]{1,0:T(8,128)(2,1)}, u32[]{:S(2)}, u32[]{:S(2)}) collective-permute-start(bf16[256,1024]{1,0:T(8,128)(2,1)} %bitcast.34), channel_id=1, source_target_pairs={{0,1},{1,0},{2,3},{3,2},{4,5},{5,4},{6,7},{7,6},{8,9},{9,8},{10,11... | collective-permute-start | bytes 1572872 | tf_op jit(solution)/shard_map/ppermute | solution.py:40
  338.3 7.3 %copy-start.2 = (bf16[72,3456]{1,0:T(8,128)(2,1)S(1)}, bf16[72,3456]{1,0:T(8,128)(2,1)}, u32[]{:S(2)}) copy-start(bf16[72,3456]{1,0:T(8,128)(2,1)} %get-tuple-element.70) | copy-start | bytes 1492996
  340.0 9.4 %copy-start.1 = (bf16[256,1152]{1,0:T(8,128)(2,1)S(1)}, bf16[256,1152]{1,0:T(8,128)(2,1)}, u32[]{:S(2)}) copy-start(bf16[256,1152]{1,0:T(8,128)(2,1)} %get-tuple-element.46) | copy-start | bytes 1769476
  343.5 6.7 %copy-start = (f32[256,1152]{1,0:T(8,128)S(1)}, f32[256,1152]{1,0:T(8,128)}, u32[]{:S(2)}) copy-start(f32[256,1152]{1,0:T(8,128)} %get-tuple-element.64) | copy-start | bytes 3538948
  345.6 5.6 %copy-start.3 = (f32[64,576]{1,0:T(8,128)S(1)}, f32[64,576]{1,0:T(8,128)}, u32[]{:S(2)}) copy-start(f32[64,576]{1,0:T(8,128)} %get-tuple-element.119) | copy-start | bytes 442372
where the time goes:
time: 352 us
  Pallas kernels  325 us (92%)
  local copies, waits for them, and re-layouts  12.8 us (4%)
  other arithmetic  9.38 us (3%)
    pallas_call x1, Pallas kernels, back(): pl.pallas_call(functools.partial(back_kernel, devices, heads, ff_pieces,...  165 us
    pallas_call x1, Pallas kernels, feed_forward(): pl.pallas_call(feed_forward_kernel, in_specs=[here] * 4 + [there] * 4, ou...  111 us
    pallas_call x1, Pallas kernels, front(): pl.pallas_call(functools.partial(front_kernel, devices, heads), in_specs=...  49.4 us
  transfers between devices with their start and end apart: 2, of which 0 were waited for; matrix products, arithmetic and copies ran while one was open for 0% of the time, Pallas kernels for 32%

commit v1 on v0

--- a/solution.py
+++ b/solution.py
@@ -460,7 +460,8 @@
         scale = lax.rsqrt(jnp.mean(value * value, -1, keepdims=True) + EPS)
         value = value * scale * gain
         first, second = value[:, : size // 2], value[:, size // 2 :]
-        cosine, sine = cos_ref[...], sin_ref[...]
+        cosine = jnp.concatenate([cos_ref[...]] * sequences, 0)
+        sine = jnp.concatenate([sin_ref[...]] * sequences, 0)
         return jnp.concatenate(
             [first * cosine - second * sine, second * cosine + first * sine], -1
         ).astype(BF16)
@@ -801,13 +802,13 @@
         )
 
     def swap_rows(kind, ref, piece):
-        first = pl.multiple_of(piece * block, block)
+        first = piece * block
         return across(
             kind, piece, ref.at[pl.ds(first, block)], ref.at[pl.ds(count + first, block)]
         )
 
     def swap_parts(kind, source, target, piece):
-        lines = pl.ds(pl.multiple_of(piece * block, block), block)
+        lines = pl.ds(piece * block, block)
         return across(kind, piece, source.at[lines], target.at[lines])
 
     def start_load(at, size, index):
@@ -832,45 +833,34 @@
     for piece in range(2):
         swap_rows(0, ff_rows, piece).start()
 
-    def forward(turn, carry):
-        b = (2 * turn) % 5 - (2 * turn) % 5 // 4
-
-        @pl.when(b >= 2)
-        def _():
-            swap_rows(0, ff_rows, b - 2).wait_recv()
-
-        lines = pl.ds(pl.multiple_of(b * block, block), block)
+    def forward(first, rows, fresh=False):
+        lines = pl.ds(first, rows)
 
         def columns(at, size, index):
-            @pl.when(b == 0)
-            def _():
+            if fresh:
                 for w in range(3):
                     load(w, at, size, index).wait()
-
             cols = pl.ds(at, size)
             g = dot(ff_rows[lines, :], gate_weight[:, cols], ((1,), (0,)))
             u = dot(ff_rows[lines, :], up_weight[:, cols], ((1,), (0,)))
-            t = jnp.tanh(GELU_SCALE * (g + GELU_CUBE * g * g * g))
-            gate[lines, cols] = g.astype(BF16)
-            upward[lines, cols] = u.astype(BF16)
-            activated[lines, cols] = (0.5 * g * (1.0 + t) * u).astype(BF16)
+            square = g * g
+            t = jnp.tanh(g * (GELU_SCALE + GELU_SCALE * GELU_CUBE * square))
+            half = 0.5 + 0.5 * t
+            gelu = g * half
+            slope = half + gelu * (1.0 - t) * (GELU_SCALE + 3.0 * GELU_SCALE * GELU_CUBE * square)
+            gate[lines, cols] = (u * slope).astype(BF16)
+            upward[lines, cols] = gelu.astype(BF16)
+            activated[lines, cols] = (gelu * u).astype(BF16)
 
         chunks(columns)
-        value = dot(activated[lines, :], down_weight[...], ((1,), (1,)))
-
-        @pl.when(b < 2)
-        def _():
-            partial[lines, :] = value
-
-        @pl.when(b >= 2)
-        def _():
-            there = pl.ds(pl.multiple_of((b - 2) * block, block), block)
-            part_send[there, :] = value.astype(BF16)
-            swap_parts(1, part_send, part_recv, b - 2).start()
-
-        return carry
-
-    lax.fori_loop(0, 4, forward, 0)
+        return dot(activated[lines, :], down_weight[...], ((1,), (1,)))
+
+    partial[...] = forward(0, count, fresh=True)
+    for piece in range(2):
+        swap_rows(0, ff_rows, piece).wait_recv()
+        there = pl.ds(piece * block, block)
+        part_send[there, :] = forward(count + piece * block, block).astype(BF16)
+        swap_parts(1, part_send, part_recv, piece).start()
     ff_turned[...] = ff_rows[...].T
     for piece in range(2):
         swap_parts(1, part_send, part_recv, piece).wait_recv()
@@ -885,46 +875,30 @@
     scale = lax.rsqrt(jnp.mean(lowered * lowered, -1, keepdims=True) + EPS)
     output_ref[...] = (hidden_ref[...] + lowered * scale * gains_ref[3:4, :]).astype(BF16)
 
-    def backward(turn, carry):
-        b = (2 * turn) % 5 - (2 * turn) % 5 // 4
-
-        @pl.when(b >= 2)
-        def _():
-            swap_rows(2, low_rows, b - 2).wait_recv()
-
-        lines = pl.ds(pl.multiple_of(b * block, block), block)
+    def backward(first, rows):
+        lines = pl.ds(first, rows)
 
         def columns(at, size, index):
             cols = pl.ds(at, size)
             d = dot(low_rows[lines, :], down_weight[:, cols], ((1,), (0,)))
-            g = gate[lines, cols].astype(F32)
-            u = upward[lines, cols].astype(F32)
-            square = g * g
-            t = jnp.tanh(GELU_SCALE * (g + GELU_CUBE * square * g))
-            half = 0.5 * (1.0 + t)
-            slope = half + 0.5 * g * (1.0 - t * t) * (
-                GELU_SCALE * (1.0 + 3.0 * GELU_CUBE * square)
-            )
-            gate[lines, cols] = (d * u * slope).astype(BF16)
-            upward[lines, cols] = (d * g * half).astype(BF16)
+            gate[lines, cols] = (d * gate[lines, cols].astype(F32)).astype(BF16)
+            upward[lines, cols] = (d * upward[lines, cols].astype(F32)).astype(BF16)
 
         chunks(columns)
+
+    def inputs_back(first):
+        lines = pl.ds(first, count)
         value = dot(gate[lines, :], gate_weight[...], ((1,), (1,)))
-        value += dot(upward[lines, :], up_weight[...], ((1,), (1,)))
-
-        @pl.when(b < 2)
-        def _():
-            partial[lines, :] = value
-
-        @pl.when(b >= 2)
-        def _():
-            there = pl.ds(pl.multiple_of((b - 2) * block, block), block)
-            back_send[there, :] = value.astype(BF16)
-            swap_parts(3, back_send, back_recv, b - 2).start()
-
-        return carry
-
-    lax.fori_loop(0, 4, backward, 0)
+        return value + dot(upward[lines, :], up_weight[...], ((1,), (1,)))
+
+    backward(0, count)
+    partial[...] = inputs_back(0)
+    for piece in range(2):
+        swap_rows(2, low_rows, piece).wait_recv()
+        backward(count + piece * block, block)
+    back_send[...] = inputs_back(count).astype(BF16)
+    for piece in range(2):
+        swap_parts(3, back_send, back_recv, piece).start()
     low_turned[...] = low_rows[...].T
 
     grads = (
@@ -1160,7 +1134,8 @@
 
     def projections():
         need("query_raw", "key_raw", "cosine", "sine", "gains")
-        cosine, sine = r["cosine"][...], r["sine"][...]
+        cosine = jnp.concatenate([r["cosine"][...]] * sequences, 0)
+        sine = jnp.concatenate([r["sine"][...]] * sequences, 0)
         gain = r["gains"][4:5, :size]
         total = jnp.zeros((1, size), F32)
         lows = []
@@ -1282,15 +1257,19 @@
 
         return run
 
+    def bring(first, last):
+        for i in range(BROUGHT.index(first), BROUGHT.index(last) + 1):
+            brought(i).start()
+
     ff.load_all(0)
-    for i in range(len(BROUGHT)):
-        brought(i).start()
     ring.enter(across=True)
     ff.give_all(0)
+    bring("att_send", "key_pos")
     ff.give_all(1)
+    ff_step(0)
     need("att_send")
     out_swap.start()
-    ff_step(0)
+    bring("att_own", BROUGHT[-1])
     need("pairs", "query", "grad_mixed", "mixed", "totals", "query_pos", "key_pos")
     lax.fori_loop(0, sequences, attention, 0)
     for step in range(chips):
@@ -1429,6 +1408,32 @@
     )(*operands)
 
 
+def finish_kernel(count, *refs):
+    sources, results = refs[:count], list(refs[count:])
+    for source in sources:
+        first = 0
+        while first < source.shape[1]:
+            result = results.pop(0)
+            result[...] = source[:, first : first + result.shape[1]].astype(result.dtype)
+            first += result.shape[1]
+
+
+def finish(sources, columns):
+    outs = [
+        jax.ShapeDtypeStruct((source.shape[0], width), kind)
+        for source, pieces in zip(sources, columns)
+        for kind, width in pieces
+    ]
+    here = pl.BlockSpec(memory_space=pltpu.VMEM)
+    return pl.pallas_call(
+        functools.partial(finish_kernel, len(sources)),
+        in_specs=[here] * len(sources),
+        out_specs=[here] * len(outs),
+        out_shape=outs,
+        name="finish",
+    )(*sources)
+
+
 def body(
     tokens,
     block_order,
@@ -1496,8 +1501,8 @@
     ) = front(
         tokens,
         own_gains,
-        jnp.tile(cosine, (sequences, 1)),
-        jnp.tile(sine, (sequences, 1)),
+        cosine,
+        sine,
         query_pos,
         key_pos,
         (weight_key, weight_value, weight_query, weight_out.T),
@@ -1538,7 +1543,6 @@
         (out_weight, weight_gate, weight_up, weight_down),
         3,
     )
-    output = output.reshape(sequences, rows, width)
 
     def both(own, other):
         return jnp.concatenate([own, other], 0)
@@ -1561,8 +1565,8 @@
         "mixed_other": swap(mixed_rows),
         "query_raw": query_raw,
         "key_raw": key_raw,
-        "cosine": jnp.tile(cosine, (sequences, 1)),
-        "sine": jnp.tile(sine, (sequences, 1)),
+        "cosine": cosine,
+        "sine": sine,
         "gains": all_gains,
         "weight_query": query_weight,
         "weight_pair": pair_weight,
@@ -1580,6 +1584,23 @@
         ]
         grad_tokens, grad_down_w, grad_gate_w, grad_up_w, grad_qkv, grad_out_w, gain_sums = back(
             given, ff_parts, heads, devices, 0
+        )
+        hidden_cols, query_cols = grad_gate_w.shape[1], heads * head_size // 2
+        (
+            output,
+            grad_tokens,
+            grad_down_w,
+            grad_gate_w,
+            grad_up_w,
+            grad_query_w,
+            grad_key_w,
+            grad_value_w,
+            grad_out_w,
+        ) = finish(
+            [output, grad_tokens, grad_down_w, grad_gate_w, grad_up_w, grad_qkv, grad_out_w],
+            [[(BF16, width)], [(F32, width)]]
+            + [[(F32, hidden_cols)]] * 3
+            + [[(F32, query_cols), (F32, local_size), (F32, local_size)], [(F32, width // 2)]],
         )
         grad_tokens = grad_tokens.reshape(sequences, rows, width)
         place = me * 2 + mine
@@ -1665,13 +1686,14 @@
             size = g.shape[0] // (2 * devices)
             outs.append(packed[first : first + size])
             first += size
-    query_cols = grad_qkv.shape[1] - 2 * local_size
-    grad_query_w = grad_qkv[:, :query_cols]
-    grad_key_w = grad_qkv[:, query_cols : query_cols + local_size]
-    grad_value_w = grad_qkv[:, query_cols + local_size :]
-    grad_down_w, grad_gate_w, grad_up_w = (
-        g.astype(F32) for g in (grad_down_w, grad_gate_w, grad_up_w)
-    )
+        query_cols = grad_qkv.shape[1] - 2 * local_size
+        grad_query_w = grad_qkv[:, :query_cols]
+        grad_key_w = grad_qkv[:, query_cols : query_cols + local_size]
+        grad_value_w = grad_qkv[:, query_cols + local_size :]
+        grad_down_w, grad_gate_w, grad_up_w = (
+            g.astype(F32) for g in (grad_down_w, grad_gate_w, grad_up_w)
+        )
+    output = output.reshape(sequences, rows, width)
     return (
         output,
         grad_tokens,

time: 352 us -> 337 us (0.957)
  Pallas kernels: 325 us -> 318 us
  local copies, waits for them, and re-layouts: 12.8 us -> 5.86 us
  other arithmetic: 9.38 us -> 4.84 us
    pallas_call x1, Pallas kernels: 111 us -> 102 us  [feed_forward(): pl.pallas_call(feed_forward_kernel, in_specs=[here] * 4 + [there] * 4, ou...]
    convert_element_type x3 -> x0, other arithmetic: 5.2 us -> none  [body(): g.astype(F32)]
    pallas_call x0 -> x1, Pallas kernels: none -> 4.36 us  [finish(): pl.pallas_call(functools.partial(finish_kernel, len(sources)), in_specs=[...]
  transfers between devices with their start and end apart: 2 -> 2, of which waited for: 0 -> 0; matrix products, arithmetic and copies ran while one was open for 0% -> 0% of each run, Pallas kernels for 32% -> 31%
where the time goes in v1:
time: 337 us; the launch traced here: 333 us
  Pallas kernels  318 us (94%)
  local copies, waits for them, and re-layouts  5.86 us (2%)
  other arithmetic  4.84 us (1%)
    pallas_call x1, Pallas kernels, back(): pl.pallas_call(functools.partial(back_kernel, devices, heads, ff_pieces,...  163 us
    pallas_call x1, Pallas kernels, feed_forward(): pl.pallas_call(feed_forward_kernel, in_specs=[here] * 4 + [there] * 4, ou...  102 us
    pallas_call x1, Pallas kernels, front(): pl.pallas_call(functools.partial(front_kernel, devices, heads), in_specs=...  49.4 us
  transfers between devices with their start and end apart: 2, of which 0 were waited for; matrix products, arithmetic and copies ran while one was open for 0% of the time, Pallas kernels for 31%

profile of v1, /device:TPU:0, one launch (start us, length us, event | category | flops | bytes accessed | tf_op | source)
XLA Modules:
  0.0 333.4 jit_solution(16285383587177372295)
XLA Ops:
  0.7 0.8 select_convert_fusion.2
  1.5 0.8 select_convert_fusion
  2.4 0.7 fusion.2
  3.2 0.7 broadcast_multiply_fusion
  3.8 1.2 dynamic_slice.21
  6.4 0.1 add_convert_fusion
  6.5 0.1 tile.21
  6.6 0.1 tile.9
  6.6 0.9 copy.31.query_pos_ref.refs_9_
  7.5 0.1 iota_add_fusion
  7.6 0.1 add.126
  7.7 0.1 add.122
  7.7 1.0 multiply_sine_fusion
  8.7 0.6 pad_add_fusion.key_pos_ref.refs_10_
  9.3 0.7 stack.46.gains_ref
  10.0 49.4 %front.1 = (bf16[16,2,128,512]{3,2,1,0:T(8,128)(2,1)}, bf16[256,1152]{1,0:T(8,128)(2,1)}, f32[256,256]{1,0:T(8,128)}, f32[256,1024]{1,0:T(8,128)}, bf16[2,128,10...) custom-call(bf16[2,128,1152]{2,1,0:T(8,128)(2,1)} %tokens_ref.1, ...), custom_call_target="tpu_custom_call" | custom-call | tf_op jit(solution)/shard_map/front/pallas_call | solution.py:597
  59.4 0.4 collective-permute-start.1
  59.8 1.7 collective-permute-start
  61.5 101.7 %feed_forward.1 = (bf16[256,1152]{1,0:T(8,128)(2,1)}, f32[256,1152]{1,0:T(8,128)}, bf16[256,1024]{1,0:T(8,128)(2,1)}, bf16[256,576]{1,0:T(8,128)(2,1)}, bf16[256...) custom-call(bf16[256,1024]{1,0:T(8,128)(2,1)} %bitcast.33, ...), custom_call_target="tpu_custom_call" | custom-call | tf_op jit(solution)/shard_map/feed_forward/pallas_call | solution.py:964
  163.2 0.0 collective-permute-done.refs_13_
  163.2 0.0 collective-permute-done.1.refs_25_
  163.2 162.9 %back.1 = (f32[256,1152]{1,0:T(8,128)}, bf16[72,3456]{1,0:T(8,128)(2,1)}, bf16[72,3456]{1,0:T(8,128)(2,1)}, bf16[72,3456]{1,0:T(8,128)(2,1)}, f32[72,768]{1,0:T(...) custom-call(bf16[16,72,3456]{2,1,0:T(8,128)(2,1)} %bitcast.26, bf16[16,72,3456]{2,1,0:T(8,128)(2,1)} %bitcast.27, ...), custom_call_target="tpu_custom_call" | custom-call | tf_op jit(solution)/shard_map/back/pallas_call | solution.py:1396
  326.1 1.5 dynamic-slice_bitcast_fusion
  327.6 1.3 fusion.1
  328.8 4.4 %finish.1 = (bf16[256,1152]{1,0:T(8,128)(2,1)}, f32[256,1152]{1,0:T(8,128)}, f32[72,3456]{1,0:T(8,128)}, f32[72,3456]{1,0:T(8,128)}, f32[72,3456]{1,0:T(8,128)},...) custom-call(bf16[256,1152]{1,0:T(8,128)(2,1)} %get-tuple-element.55.refs_0_, ...), custom_call_target="tpu_custom_call" | custom-call | tf_op jit(solution)/shard_map/finish/pallas_call | solution.py:1428
  (14 shorter events, 0.1 us)
Async XLA Ops:
  59.4 103.8 %collective-permute-start.1 = (bf16[256,1152]{1,0:T(8,128)(2,1)}, bf16[256,1152]{1,0:T(8,128)(2,1)}, u32[]{:S(2)}, u32[]{:S(2)}) collective-permute-start(bf16[256,1152]{1,0:T(8,128)(2,1)} %get-tuple-element.72.refs_24_), channel_id=1, source_target_pairs={{0,1},{1,0},{2,3},{3,2},{4,5},{5,4},{6,7},{7,6},{8,9},{9,8},{10,11... | collective-permute-start | bytes 1769480 | tf_op jit(solution)/shard_map/ppermute | solution.py:40
  59.8 103.4 %collective-permute-start = (bf16[256,1024]{1,0:T(8,128)(2,1)}, bf16[256,1024]{1,0:T(8,128)(2,1)}, u32[]{:S(2)}, u32[]{:S(2)}) collective-permute-start(bf16[256,1024]{1,0:T(8,128)(2,1)} %bitcast.32), channel_id=1, source_target_pairs={{0,1},{1,0},{2,3},{3,2},{4,5},{5,4},{6,7},{7,6},{8,9},{9,8},{10,11... | collective-permute-start | bytes 1572872 | tf_op jit(solution)/shard_map/ppermute | solution.py:40

commit v2 on v1

--- a/solution.py
+++ b/solution.py
@@ -344,19 +344,25 @@
     value_weight,
     query_weight,
     out_weight,
-    pairs_ref,
     normed_ref,
     key_ref,
-    query_ref,
     query_low_ref,
     mixed_low_ref,
     mixed_ref,
     totals_ref,
     all_gains_ref,
+    pairs_hbm,
+    query_hbm,
+    pair_whole_hbm,
+    query_whole_hbm,
+    out_whole_hbm,
+    pairs_ref,
+    query_ref,
     pair_whole,
     query_whole,
     out_whole,
     gains_other,
+    keep_sem,
     own_sem,
     cross_send,
     cross_recv,
@@ -386,6 +392,16 @@
         start = side * cols + (size if i == 1 else 0)
         target = query_whole if i == 2 else pair_whole
         return target.at[pl.ds(pl.multiple_of(first, 16), lines), pl.ds(pl.multiple_of(start, 128), cols)]
+
+    def keep(i):
+        source, target = (
+            (pairs_ref, pairs_hbm),
+            (query_ref, query_hbm),
+            (pair_whole, pair_whole_hbm),
+            (query_whole, query_whole_hbm),
+            (out_whole, out_whole_hbm),
+        )[i]
+        return pltpu.make_async_copy(source, target, keep_sem.at[i])
 
     def own(i):
         return pltpu.make_async_copy(
@@ -534,6 +550,7 @@
     for i in (0, 1):
         own(i).wait()
         side(i).wait_recv()
+    keep(2).start()
     value = dot(normed_ref[...], pair_whole[...], ((1,), (0,)))
     key_ref[...] = value[:, :size]
     key_low = turned(value[:, :size], all_gains_ref[4:5, size : 2 * size])
@@ -548,13 +565,19 @@
         if hop == 2:
             own(2).wait()
             side(2).wait_recv()
+            keep(3).start()
             queries()
+            keep(1).start()
     cross(3).wait_recv()
     side(3).start()
     for hop in range(far + 1):
         for way, seq in streams:
             if hop <= hops(way, seq) and (hop > 0 or way > 0):
                 twin(way, seq, hop).wait_recv()
+    keep(0).start()
+    own(3).wait()
+    side(3).wait_recv()
+    keep(4).start()
     lax.fori_loop(0, sequences, attention, 0)
     for hop in range(far + 1):
         for way, seq in streams:
@@ -564,12 +587,12 @@
                 twin(way, seq, hop).wait_send()
             if hop < hops(way, seq):
                 flow(way, seq, hop).wait_send()
-    own(3).wait()
-    side(3).wait_recv()
     for i in order:
         cross(i).wait_send()
     for i in range(len(weights)):
         side(i).wait_send()
+    for i in range(5):
+        keep(i).wait()
 
 
 def front(tokens, gains, cosine, sine, query_pos, key_pos, weights, heads, devices, collective_id):
@@ -581,15 +604,17 @@
     here, there = pl.BlockSpec(memory_space=pltpu.VMEM), pl.BlockSpec(memory_space=pl.ANY)
     streams = pltpu.SemaphoreType.DMA((2 * sequences, far + 1))
     outs = [
-        ((devices, sequences, rows, 2 * size), BF16),
         ((count, width), BF16),
         ((count, size), F32),
-        ((count, heads * size), F32),
         ((sequences, rows, heads * size), BF16),
         ((sequences, rows, heads * size), BF16),
         ((sequences, stacked, size), F32),
         ((sequences, stacked, 128), F32),
         (gains.shape, F32),
+    ]
+    kept = [
+        ((devices, sequences, rows, 2 * size), BF16),
+        ((count, heads * size), F32),
         ((width, 2 * size), BF16),
         ((width, heads * size), BF16),
         ((width, heads * size), BF16),
@@ -597,9 +622,11 @@
     return pl.pallas_call(
         functools.partial(front_kernel, devices, heads),
         in_specs=[here] * 6 + [there] * 4,
-        out_specs=[here] * len(outs),
-        out_shape=[jax.ShapeDtypeStruct(shape, kind) for shape, kind in outs],
-        scratch_shapes=[pltpu.VMEM(gains.shape, gains.dtype)]
+        out_specs=[here] * len(outs) + [there] * len(kept),
+        out_shape=[jax.ShapeDtypeStruct(shape, kind) for shape, kind in outs + kept],
+        scratch_shapes=[pltpu.VMEM(shape, kind) for shape, kind in kept]
+        + [pltpu.VMEM(gains.shape, gains.dtype)]
+        + [pltpu.SemaphoreType.DMA((5,))]
         + [pltpu.SemaphoreType.DMA((4,))]
         + [pltpu.SemaphoreType.DMA((5,))] * 2
         + [pltpu.SemaphoreType.DMA((4,))] * 2
@@ -803,12 +830,11 @@
 
     def swap_rows(kind, ref, piece):
         first = piece * block
-        return across(
-            kind, piece, ref.at[pl.ds(first, block)], ref.at[pl.ds(count + first, block)]
-        )
+        here, there = pl.multiple_of(first, block), pl.multiple_of(count + first, block)
+        return across(kind, piece, ref.at[pl.ds(here, block)], ref.at[pl.ds(there, block)])
 
     def swap_parts(kind, source, target, piece):
-        lines = pl.ds(piece * block, block)
+        lines = pl.ds(pl.multiple_of(piece * block, block), block)
         return across(kind, piece, source.at[lines], target.at[lines])
 
     def start_load(at, size, index):
@@ -833,13 +859,19 @@
     for piece in range(2):
         swap_rows(0, ff_rows, piece).start()
 
-    def forward(first, rows, fresh=False):
-        lines = pl.ds(first, rows)
+    def forward(b, carry):
+        @pl.when(b >= 2)
+        def _():
+            swap_rows(0, ff_rows, b - 2).wait_recv()
+
+        lines = pl.ds(pl.multiple_of(b * block, block), block)
 
         def columns(at, size, index):
-            if fresh:
+            @pl.when(b == 0)
+            def _():
                 for w in range(3):
                     load(w, at, size, index).wait()
+
             cols = pl.ds(at, size)
             g = dot(ff_rows[lines, :], gate_weight[:, cols], ((1,), (0,)))
             u = dot(ff_rows[lines, :], up_weight[:, cols], ((1,), (0,)))
@@ -853,14 +885,22 @@
             activated[lines, cols] = (gelu * u).astype(BF16)
 
         chunks(columns)
-        return dot(activated[lines, :], down_weight[...], ((1,), (1,)))
-
-    partial[...] = forward(0, count, fresh=True)
-    for piece in range(2):
-        swap_rows(0, ff_rows, piece).wait_recv()
-        there = pl.ds(piece * block, block)
-        part_send[there, :] = forward(count + piece * block, block).astype(BF16)
-        swap_parts(1, part_send, part_recv, piece).start()
+
+        @pl.when(b == 1)
+        def _():
+            partial[...] = dot(activated[:count, :], down_weight[...], ((1,), (1,)))
+
+        @pl.when(b >= 2)
+        def _():
+            there = pl.ds(pl.multiple_of((b - 2) * block, block), block)
+            part_send[there, :] = dot(activated[lines, :], down_weight[...], ((1,), (1,))).astype(
+                BF16
+            )
+            swap_parts(1, part_send, part_recv, b - 2).start()
+
+        return carry
+
+    lax.fori_loop(0, 4, forward, 0)
     ff_turned[...] = ff_rows[...].T
     for piece in range(2):
         swap_parts(1, part_send, part_recv, piece).wait_recv()
@@ -875,30 +915,41 @@
     scale = lax.rsqrt(jnp.mean(lowered * lowered, -1, keepdims=True) + EPS)
     output_ref[...] = (hidden_ref[...] + lowered * scale * gains_ref[3:4, :]).astype(BF16)
 
-    def backward(first, rows):
-        lines = pl.ds(first, rows)
-
-        def columns(at, size, index):
-            cols = pl.ds(at, size)
-            d = dot(low_rows[lines, :], down_weight[:, cols], ((1,), (0,)))
-            gate[lines, cols] = (d * gate[lines, cols].astype(F32)).astype(BF16)
-            upward[lines, cols] = (d * upward[lines, cols].astype(F32)).astype(BF16)
-
-        chunks(columns)
-
-    def inputs_back(first):
-        lines = pl.ds(first, count)
+    def backward(half, carry):
+        def columns_of(piece, carry):
+            @pl.when(half == 1)
+            def _():
+                swap_rows(2, low_rows, piece).wait_recv()
+
+            lines = pl.ds(pl.multiple_of(half * count + piece * block, block), block)
+
+            def columns(at, size, index):
+                cols = pl.ds(at, size)
+                d = dot(low_rows[lines, :], down_weight[:, cols], ((1,), (0,)))
+                gate[lines, cols] = (d * gate[lines, cols].astype(F32)).astype(BF16)
+                upward[lines, cols] = (d * upward[lines, cols].astype(F32)).astype(BF16)
+
+            chunks(columns)
+            return carry
+
+        lax.fori_loop(0, 2, columns_of, 0)
+        lines = pl.ds(pl.multiple_of(half * count, block), count)
         value = dot(gate[lines, :], gate_weight[...], ((1,), (1,)))
-        return value + dot(upward[lines, :], up_weight[...], ((1,), (1,)))
-
-    backward(0, count)
-    partial[...] = inputs_back(0)
-    for piece in range(2):
-        swap_rows(2, low_rows, piece).wait_recv()
-        backward(count + piece * block, block)
-    back_send[...] = inputs_back(count).astype(BF16)
-    for piece in range(2):
-        swap_parts(3, back_send, back_recv, piece).start()
+        value += dot(upward[lines, :], up_weight[...], ((1,), (1,)))
+
+        @pl.when(half == 0)
+        def _():
+            partial[...] = value
+
+        @pl.when(half == 1)
+        def _():
+            back_send[...] = value.astype(BF16)
+            for piece in range(2):
+                swap_parts(3, back_send, back_recv, piece).start()
+
+        return carry
+
+    lax.fori_loop(0, 2, backward, 0)
     low_turned[...] = low_rows[...].T
 
     grads = (
@@ -1066,6 +1117,8 @@
     out_swap = across(0, r["att_send"], r["att_across"])
     col_swap = across(1, r["col_send"], r["col_rows"].at[pl.ds(count, count)])
     gain_swap = across(2, r["gain_own"], r["gain_across"])
+    mixed_swap = across(3, r["mixed_own"], r["mixed_other"])
+    normed_swap = across(4, r["normed_own"], r["normed_other"])
     gain_twin = pltpu.make_async_remote_copy(
         src_ref=r["gain_pair"],
         dst_ref=r["gain_twin"],
@@ -1184,15 +1237,16 @@
         gain_swap.start()
 
     def out_part():
-        need("mixed_own", "mixed_other", "att_own")
+        need("att_own")
         out_swap.wait_recv()
+        mixed_swap.wait_recv()
         _, lines, cols = r["out_part"].shape
         value = dot(r["mixed_own"][...], r["att_own"][...], ((0,), (0,)))
         value += dot(r["mixed_other"][...], r["att_across"][...], ((0,), (0,)))
         r["out_part"][...] = value.reshape(devices, lines, cols).astype(BF16)
 
     def turn_rows():
-        need("normed_own", "normed_other")
+        normed_swap.wait_recv()
         r["weight_pair"][:, :count] = r["normed_own"][...].T
         r["weight_pair"][:, count:] = r["normed_other"][...].T
 
@@ -1269,7 +1323,10 @@
     ff_step(0)
     need("att_send")
     out_swap.start()
-    bring("att_own", BROUGHT[-1])
+    bring("mixed_own", BROUGHT[-1])
+    need("mixed_own", "normed_own")
+    mixed_swap.start()
+    normed_swap.start()
     need("pairs", "query", "grad_mixed", "mixed", "totals", "query_pos", "key_pos")
     lax.fori_loop(0, sequences, attention, 0)
     for step in range(chips):
@@ -1286,7 +1343,7 @@
     ff_step(6, [attn_step(3), attn_step(4), attn_step(5)])
     ff_step(7, [attn_step(6), attn_step(7)])
     r["gains_total"][...] = r["gain_sum"][...]
-    for copy in (out_swap, col_swap, gain_swap, gain_twin):
+    for copy in (out_swap, col_swap, gain_swap, mixed_swap, normed_swap, gain_twin):
         copy.wait_send()
     for way in range(2):
         for step in range(gain_hops[way]):
@@ -1305,9 +1362,9 @@
     "totals",
     "query_pos",
     "key_pos",
+    "mixed_own",
+    "normed_own",
     "att_own",
-    "mixed_own",
-    "mixed_other",
     "query_raw",
     "key_raw",
     "cosine",
@@ -1318,8 +1375,6 @@
     "tokens",
     "grad_hidden",
     "gain_part",
-    "normed_own",
-    "normed_other",
 )
 
 
@@ -1375,6 +1430,8 @@
     scratch["kv_other"] = slots(chips, given["pairs"])
     scratch["kv_flow"] = slots(chips, given["pairs"])
     scratch["kv_sum"] = pltpu.VMEM((pair_rows, 2 * size), F32)
+    for name in ("mixed", "normed"):
+        scratch[f"{name}_other"] = pltpu.VMEM(given[f"{name}_own"].shape, BF16)
     scratch["att_across"] = pltpu.VMEM((count, out_cols), BF16)
     scratch["query_low"] = pltpu.VMEM((count, heads * size), BF16)
     scratch["pair_low"] = pltpu.VMEM((count, 2 * size), BF16)
@@ -1388,7 +1445,7 @@
         scratch[name] = pltpu.VMEM(given["gains"].shape, F32)
     scratch["gain_flow"] = pltpu.VMEM((2, chips // 2 + 1) + given["gains"].shape, F32)
     scratch["bring"] = dma(len(BROUGHT))
-    for name, n in (("cross_send", 3), ("cross_recv", 3), ("twin_send", 1), ("twin_recv", 1)):
+    for name, n in (("cross_send", 5), ("cross_recv", 5), ("twin_send", 1), ("twin_recv", 1)):
         scratch[name] = dma(n)
     scratch["gain_send"] = dma(2, chips // 2)
     scratch["gain_recv"] = dma(2, chips // 2)
@@ -1486,15 +1543,15 @@
     own_gains.append(jnp.concatenate(small + [jnp.zeros((width - 2 * head_size,), F32)]))
     own_gains = jnp.stack(own_gains + [jnp.zeros((width,), F32)] * 3)
     (
-        pairs,
         normed_rows,
         key_raw,
-        query_raw,
         query_low,
         mixed_low,
         mixed,
         totals,
         all_gains,
+        pairs,
+        query_raw,
         pair_weight,
         query_weight,
         out_weight,
@@ -1562,7 +1619,6 @@
         "query_pos": query_pos,
         "key_pos": key_pos,
         "mixed_own": mixed_rows,
-        "mixed_other": swap(mixed_rows),
         "query_raw": query_raw,
         "key_raw": key_raw,
         "cosine": cosine,
@@ -1574,7 +1630,6 @@
         "grad_hidden": grad_hidden.reshape(count, width),
         "gain_part": gain_part,
         "normed_own": normed_rows,
-        "normed_other": swap(normed_rows),
     }
     aligned = width % (8 * devices) == 0 and mixed_rows.shape[1] % (32 * devices) == 0
     if aligned and count == head_size:

time: 337 us -> 314 us (0.932)
  Pallas kernels: 318 us -> 301 us
    pallas_call x1, Pallas kernels: 102 us -> 87.1 us  [feed_forward(): pl.pallas_call(feed_forward_kernel, in_specs=[here] * 4 + [there] * 4, ou...]
  transfers between devices with their start and end apart: 2 -> 0, of which waited for: 0 -> 0; matrix products, arithmetic and copies ran while one was open for 0% -> 0% of each run, Pallas kernels for 31% -> 0%
where the time goes in v2:
time: 314 us; the launch traced here: 313 us
  Pallas kernels  301 us (96%)
  local copies, waits for them, and re-layouts  5.85 us (2%)
  other arithmetic  4.84 us (2%)
    pallas_call x1, Pallas kernels, back(): pl.pallas_call(functools.partial(back_kernel, devices, heads, ff_pieces,...  163 us
    pallas_call x1, Pallas kernels, feed_forward(): pl.pallas_call(feed_forward_kernel, in_specs=[here] * 4 + [there] * 4, ou...  87.1 us
    pallas_call x1, Pallas kernels, front(): pl.pallas_call(functools.partial(front_kernel, devices, heads), in_specs=...  46.6 us

profile of v2, /device:TPU:0, one launch (start us, length us, event | category | flops | bytes accessed | tf_op | source)
XLA Modules:
  0.0 313.4 jit_solution(6028488014454235916)
XLA Ops:
  0.7 0.8 select_convert_fusion.2
  1.5 0.8 select_convert_fusion
  2.4 0.7 fusion.2
  3.2 0.7 stack.46.gains_ref
  3.9 1.2 dynamic_slice.21
  6.4 0.1 add_convert_fusion
  6.5 1.0 multiply_sine_fusion
  7.5 0.1 tile.21
  7.5 0.1 tile.9
  7.6 0.9 copy.31.query_pos_ref.refs_9_
  8.5 0.7 broadcast_multiply_fusion
  9.2 0.1 iota_add_fusion
  9.2 0.1 add.126
  9.3 0.1 add.122
  9.4 0.6 pad_add_fusion.key_pos_ref.refs_10_
  10.0 46.6 %front.1 = (bf16[256,1152]{1,0:T(8,128)(2,1)}, f32[256,256]{1,0:T(8,128)}, bf16[2,128,1024]{2,1,0:T(8,128)(2,1)}, bf16[2,128,1024]{2,1,0:T(8,128)(2,1)}, f32[2,5...) custom-call(bf16[2,128,1152]{2,1,0:T(8,128)(2,1)} %tokens_ref.1, ...), custom_call_target="tpu_custom_call" | custom-call | tf_op jit(solution)/shard_map/front/pallas_call | solution.py:622
  56.6 87.1 %feed_forward.1 = (bf16[256,1152]{1,0:T(8,128)(2,1)}, f32[256,1152]{1,0:T(8,128)}, bf16[256,1024]{1,0:T(8,128)(2,1)}, bf16[256,576]{1,0:T(8,128)(2,1)}, bf16[256...) custom-call(bf16[256,1024]{1,0:T(8,128)(2,1)} %bitcast.32, ...), custom_call_target="tpu_custom_call" | custom-call | tf_op jit(solution)/shard_map/feed_forward/pallas_call | solution.py:1015
  143.8 162.5 %back.1 = (f32[256,1152]{1,0:T(8,128)}, bf16[72,3456]{1,0:T(8,128)(2,1)}, bf16[72,3456]{1,0:T(8,128)(2,1)}, bf16[72,3456]{1,0:T(8,128)(2,1)}, f32[72,768]{1,0:T(...) custom-call(bf16[16,72,3456]{2,1,0:T(8,128)(2,1)} %bitcast.26, bf16[16,72,3456]{2,1,0:T(8,128)(2,1)} %bitcast.27, ...), custom_call_target="tpu_custom_call" | custom-call | tf_op jit(solution)/shard_map/back/pallas_call | solution.py:1453
  306.3 4.4 %finish.1 = (bf16[256,1152]{1,0:T(8,128)(2,1)}, f32[256,1152]{1,0:T(8,128)}, f32[72,3456]{1,0:T(8,128)}, f32[72,3456]{1,0:T(8,128)}, f32[72,3456]{1,0:T(8,128)},...) custom-call(bf16[256,1152]{1,0:T(8,128)(2,1)} %get-tuple-element.55.refs_0_, ...), custom_call_target="tpu_custom_call" | custom-call | tf_op jit(solution)/shard_map/finish/pallas_call | solution.py:1485
  310.7 1.4 dynamic-slice_bitcast_fusion
  312.2 1.3 fusion.1
  (14 shorter events, 0.1 us)

commit v3 on v2

--- a/solution.py
+++ b/solution.py
@@ -1185,13 +1185,12 @@
         middle = value.shape[1] // 2
         return jnp.where(which == 0, value[:, :middle], value[:, middle:])
 
-    def projections():
-        need("query_raw", "key_raw", "cosine", "sine", "gains")
+    def query_grads():
+        need("query_raw", "cosine", "sine", "gains")
         cosine = jnp.concatenate([r["cosine"][...]] * sequences, 0)
         sine = jnp.concatenate([r["sine"][...]] * sequences, 0)
         gain = r["gains"][4:5, :size]
         total = jnp.zeros((1, size), F32)
-        lows = []
         for h in range(heads):
             cols = slice(h * size, (h + 1) * size)
             grad = jnp.concatenate(
@@ -1202,11 +1201,17 @@
                 ],
                 0,
             )
-            back, part = norm_back(
+            value, part = norm_back(
                 turn_back(grad, cosine, sine), r["query_raw"][:, cols], gain
             )
             total += part
-            r["query_low"][:, cols] = back.astype(BF16)
+            r["query_low"][:, cols] = value.astype(BF16)
+        r["gain_sum"][4:5, :size] = total
+
+    def projections():
+        need("key_raw")
+        cosine = jnp.concatenate([r["cosine"][...]] * sequences, 0)
+        sine = jnp.concatenate([r["sine"][...]] * sequences, 0)
         back, key_total = norm_back(
             turn_back(r["kv_sum"][:, :size], cosine, sine),
             r["key_raw"][...],
@@ -1232,7 +1237,7 @@
         r["grad_tokens"][...] = back + r["grad_hidden"][...]
         r["gain_own"][...] = r["gain_part"][...]
         r["gain_own"][0:1, :] = part
-        r["gain_own"][4:5, :size] = total
+        r["gain_own"][4:5, :size] = r["gain_sum"][4:5, :size]
         r["gain_own"][4:5, size : 2 * size] = key_total
         gain_swap.start()
 
@@ -1332,7 +1337,7 @@
     for step in range(chips):
         kv.give_all(step)
     ff_step(1, [kv_step(0), kv_step(1), kv_step(2)])
-    ff_step(2, [kv_step(3), kv_step(4), kv_step(5)])
+    ff_step(2, [kv_step(3), kv_step(4), kv_step(5), query_grads])
     ff_step(3, [kv_step(6), kv_step(7), out_part])
     projections()
     ff_step(4, [turn_rows])

time: 314 us -> 314 us (level)
  no operation moved by 1% of the time
where the time goes in v3:
time: 314 us; the launch traced here: 313 us
  Pallas kernels  301 us (96%)
  local copies, waits for them, and re-layouts  5.85 us (2%)
  other arithmetic  4.84 us (2%)
    pallas_call x1, Pallas kernels, back(): pl.pallas_call(functools.partial(back_kernel, devices, heads, ff_pieces,...  163 us
    pallas_call x1, Pallas kernels, feed_forward(): pl.pallas_call(feed_forward_kernel, in_specs=[here] * 4 + [there] * 4, ou...  87.1 us
    pallas_call x1, Pallas kernels, front(): pl.pallas_call(functools.partial(front_kernel, devices, heads), in_specs=...  46.6 us

profile of v3, /device:TPU:0, one launch (start us, length us, event | category | flops | bytes accessed | tf_op | source)
XLA Modules:
  0.0 313.4 jit_solution(16328177928227088815)
XLA Ops:
  0.7 0.8 select_convert_fusion.2
  1.5 0.8 select_convert_fusion
  2.4 0.7 fusion.2
  3.2 0.7 stack.46.gains_ref
  3.9 1.2 dynamic_slice.21
  6.4 0.1 add_convert_fusion
  6.5 1.0 multiply_sine_fusion
  7.5 0.1 tile.21
  7.5 0.1 tile.9
  7.6 0.9 copy.31.query_pos_ref.refs_9_
  8.5 0.7 broadcast_multiply_fusion
  9.2 0.1 iota_add_fusion
  9.2 0.1 add.126
  9.3 0.1 add.122
  9.4 0.6 pad_add_fusion.key_pos_ref.refs_10_
  10.0 46.6 %front.1 = (bf16[256,1152]{1,0:T(8,128)(2,1)}, f32[256,256]{1,0:T(8,128)}, bf16[2,128,1024]{2,1,0:T(8,128)(2,1)}, bf16[2,128,1024]{2,1,0:T(8,128)(2,1)}, f32[2,5...) custom-call(bf16[2,128,1152]{2,1,0:T(8,128)(2,1)} %tokens_ref.1, ...), custom_call_target="tpu_custom_call" | custom-call | tf_op jit(solution)/shard_map/front/pallas_call | solution.py:622
  56.6 87.1 %feed_forward.1 = (bf16[256,1152]{1,0:T(8,128)(2,1)}, f32[256,1152]{1,0:T(8,128)}, bf16[256,1024]{1,0:T(8,128)(2,1)}, bf16[256,576]{1,0:T(8,128)(2,1)}, bf16[256...) custom-call(bf16[256,1024]{1,0:T(8,128)(2,1)} %bitcast.32, ...), custom_call_target="tpu_custom_call" | custom-call | tf_op jit(solution)/shard_map/feed_forward/pallas_call | solution.py:1015
  143.8 162.5 %back.1 = (f32[256,1152]{1,0:T(8,128)}, bf16[72,3456]{1,0:T(8,128)(2,1)}, bf16[72,3456]{1,0:T(8,128)(2,1)}, bf16[72,3456]{1,0:T(8,128)(2,1)}, f32[72,768]{1,0:T(...) custom-call(bf16[16,72,3456]{2,1,0:T(8,128)(2,1)} %bitcast.26, bf16[16,72,3456]{2,1,0:T(8,128)(2,1)} %bitcast.27, ...), custom_call_target="tpu_custom_call" | custom-call | tf_op jit(solution)/shard_map/back/pallas_call | solution.py:1458
  306.3 4.4 %finish.1 = (bf16[256,1152]{1,0:T(8,128)(2,1)}, f32[256,1152]{1,0:T(8,128)}, f32[72,3456]{1,0:T(8,128)}, f32[72,3456]{1,0:T(8,128)}, f32[72,3456]{1,0:T(8,128)},...) custom-call(bf16[256,1152]{1,0:T(8,128)(2,1)} %get-tuple-element.55.refs_0_, ...), custom_call_target="tpu_custom_call" | custom-call | tf_op jit(solution)/shard_map/finish/pallas_call | solution.py:1490
  310.7 1.4 dynamic-slice_bitcast_fusion
  312.2 1.3 fusion.1
  (14 shorter events, 0.1 us)

commit v4 on v2

--- a/solution.py
+++ b/solution.py
@@ -1390,7 +1390,7 @@
     ff_pieces = split_ways(ff_parts)
     pair_rows = given["pairs"].shape[1]
     kv_pieces = tuple(
-        (0, 1 - 2 * i, i * pair_rows // 2, pair_rows // 2, 0, 2 * size) for i in range(2)
+        (0, 1 - 2 * (i % 2), i * pair_rows // 4, pair_rows // 4, 0, 2 * size) for i in range(4)
     )
     attn_pieces = (
         (0, 1, 0, lines, 0, cols // 2),

time: 314 us -> 314 us (level)
  no operation moved by 1% of the time
where the time goes in v4:
time: 314 us
  Pallas kernels  301 us (96%)
  local copies, waits for them, and re-layouts  5.85 us (2%)
  other arithmetic  4.84 us (2%)
    pallas_call x1, Pallas kernels, back(): pl.pallas_call(functools.partial(back_kernel, devices, heads, ff_pieces,...  163 us
    pallas_call x1, Pallas kernels, feed_forward(): pl.pallas_call(feed_forward_kernel, in_specs=[here] * 4 + [there] * 4, ou...  87.1 us
    pallas_call x1, Pallas kernels, front(): pl.pallas_call(functools.partial(front_kernel, devices, heads), in_specs=...  46.6 us

profile of v4, /device:TPU:0, one launch (start us, length us, event | category | flops | bytes accessed | tf_op | source)
XLA Modules:
  0.0 314.0 jit_solution(7879544131197873479)
XLA Ops:
  0.7 0.8 select_convert_fusion.2
  1.5 0.8 select_convert_fusion
  2.4 0.7 fusion.2
  3.2 0.7 stack.46.gains_ref
  3.9 1.2 dynamic_slice.21
  6.4 0.1 add_convert_fusion
  6.5 1.0 multiply_sine_fusion
  7.5 0.1 tile.21
  7.5 0.1 tile.9
  7.6 0.9 copy.31.query_pos_ref.refs_9_
  8.5 0.7 broadcast_multiply_fusion
  9.2 0.1 iota_add_fusion
  9.2 0.1 add.126
  9.3 0.1 add.122
  9.4 0.6 pad_add_fusion.key_pos_ref.refs_10_
  10.0 46.6 %front.1 = (bf16[256,1152]{1,0:T(8,128)(2,1)}, f32[256,256]{1,0:T(8,128)}, bf16[2,128,1024]{2,1,0:T(8,128)(2,1)}, bf16[2,128,1024]{2,1,0:T(8,128)(2,1)}, f32[2,5...) custom-call(bf16[2,128,1152]{2,1,0:T(8,128)(2,1)} %tokens_ref.1, ...), custom_call_target="tpu_custom_call" | custom-call | tf_op jit(solution)/shard_map/front/pallas_call | solution.py:622
  56.6 87.1 %feed_forward.1 = (bf16[256,1152]{1,0:T(8,128)(2,1)}, f32[256,1152]{1,0:T(8,128)}, bf16[256,1024]{1,0:T(8,128)(2,1)}, bf16[256,576]{1,0:T(8,128)(2,1)}, bf16[256...) custom-call(bf16[256,1024]{1,0:T(8,128)(2,1)} %bitcast.32, ...), custom_call_target="tpu_custom_call" | custom-call | tf_op jit(solution)/shard_map/feed_forward/pallas_call | solution.py:1015
  143.8 163.1 %back.1 = (f32[256,1152]{1,0:T(8,128)}, bf16[72,3456]{1,0:T(8,128)(2,1)}, bf16[72,3456]{1,0:T(8,128)(2,1)}, bf16[72,3456]{1,0:T(8,128)(2,1)}, f32[72,768]{1,0:T(...) custom-call(bf16[16,72,3456]{2,1,0:T(8,128)(2,1)} %bitcast.26, bf16[16,72,3456]{2,1,0:T(8,128)(2,1)} %bitcast.27, ...), custom_call_target="tpu_custom_call" | custom-call | tf_op jit(solution)/shard_map/back/pallas_call | solution.py:1453
  306.9 4.4 %finish.1 = (bf16[256,1152]{1,0:T(8,128)(2,1)}, f32[256,1152]{1,0:T(8,128)}, f32[72,3456]{1,0:T(8,128)}, f32[72,3456]{1,0:T(8,128)}, f32[72,3456]{1,0:T(8,128)},...) custom-call(bf16[256,1152]{1,0:T(8,128)(2,1)} %get-tuple-element.55.refs_0_, ...), custom_call_target="tpu_custom_call" | custom-call | tf_op jit(solution)/shard_map/finish/pallas_call | solution.py:1485
  311.3 1.4 dynamic-slice_bitcast_fusion
  312.7 1.3 fusion.1
  (14 shorter events, 0.1 us)
